TPU v7x, 768 devices: a whole 4x8x12 slice. The times are simulated.
768 devices in a mesh: dp: 96 (over z, x, core), mp: 8 (over y).
Axes of the slice: x: 4, y: 8, z: 12, core: 2. Of those that a mesh axis runs over, the one named last changes fastest.
Arguments:
- vision_rows: bfloat16 [24576, 1024], P('dp'), may hold values from -6 to 6
- image_count: int32 [768], P('dp'), may hold values from 0 to 4
- proj_flat: bfloat16 [36864, 128], P(('dp', 'mp')), may hold values from -0.1875 to 0.1875
- text_embeds: bfloat16 [73728, 4096], P(('dp', 'mp')), may hold values from -6 to 6
- norm_gain: float32 [4096], replicated, may hold values from 0.1 to 1.9
- q_weight: bfloat16 [4096, 4096], P(None, 'mp'), may hold values from -0.09375 to 0.09375
- q_grad: bfloat16 [98304, 4096], P('dp', 'mp'), may hold values from -6 to 6
Outputs:
- text_grad: bfloat16 [73728, 4096], P(('dp', 'mp'))
- proj_grad: float32 [36864, 128], P(('dp', 'mp'))
Inputs may be any that keep to these rules, and one draw needn't show every extreme that they name: Slot s of device k holds an image when s < image_count[k]; other slots are padding.
All inputs are finite; a program needn't handle non-finite values.
Results may differ from a plain program's by a relative error of at most 0.014.
Values may be sent and summed in bfloat16 or wider, within the bound.
No kernel may reach another device: no remote copies, remote signals or barrier semaphores. Data moves between devices by JAX's collectives and lax.ppermute only.
A program may use at most 64 MiB of HBM per device.

v0:
```python
import jax
import jax.numpy as jnp
from jax import lax
from jax.sharding import Mesh
from jax.sharding import PartitionSpec as P

IMG_MAX = 4
PATCH = 8
DP = ("dp_0", "dp_1", "dp_2")
DP_MP = ("dp_0", "dp_1", "dp_2", "mp")


norm_eps = 1e-05


def own_block(blocks, axes, sequence):
    dims = [lax.axis_size(a) for a in axes]
    blocks = blocks.reshape(*dims, *blocks.shape[1:])
    blocks = blocks.transpose(*sequence, *range(len(axes), blocks.ndim))
    blocks = blocks.reshape(-1, *blocks.shape[len(axes) :])
    for k in sequence:
        blocks = lax.psum_scatter(blocks, axes[k], scatter_dimension=0, tiled=True)
    return blocks[0]


def in_blocks(array, dim, count):
    dims = array.shape
    blocks = array.reshape(*dims[:dim], count, dims[dim] // count, *dims[dim + 1 :])
    return jnp.moveaxis(blocks, dim, 0)


def summed_rows(array, axes, sequence, dim):
    count = lax.axis_size(axes)
    return own_block(in_blocks(array, dim, count), axes, sequence)


def row_term(left, weight):
    return lax.dot_general(
        left, weight, (((1,), (1,)), ((), ())), preferred_element_type=jnp.float32
    )


def norm_back(rows_in, grads, gain):
    inputs = rows_in.astype(jnp.float32)
    inv_rms = lax.rsqrt(jnp.mean(inputs * inputs, axis=-1, keepdims=True) + norm_eps)
    scaled = gain[None, :] * grads
    inner_mean = jnp.mean(scaled * inputs, axis=-1, keepdims=True)
    return inv_rms * scaled - inputs * inv_rms**3 * inner_mean


def body(vision_rows, image_count, proj_flat, text_embeds, norm_gain, q_weight, q_grad):
    groups = lax.axis_size("mp")
    member = lax.axis_index("mp")
    shards = lax.axis_size(DP)
    enc_width = vision_rows.shape[1]
    block_cols = q_weight.shape[1]
    used_count = enc_width * block_cols
    image_rows = IMG_MAX * PATCH
    gathered = lax.all_gather(proj_flat, DP, axis=0, tiled=True)
    proj_block = gathered.reshape(-1)[:used_count].reshape(enc_width, block_cols)
    embed_cols = jnp.dot(vision_rows, proj_block, preferred_element_type=jnp.float32).astype(
        jnp.bfloat16
    )
    row_ids = jnp.arange(groups * image_rows, dtype=jnp.int32)
    owners = row_ids // image_rows
    slot_ids = row_ids % image_rows // PATCH
    owner_match = owners[:, None] == jnp.arange(groups, dtype=jnp.int32)[None, :]
    owner_counts = jnp.sum(jnp.where(owner_match, image_count[None, :], 0), axis=1)
    live_group = (slot_ids < owner_counts)[:, None]
    norm_grad = lax.psum_scatter(
        row_term(q_grad, q_weight).astype(jnp.bfloat16), "mp", scatter_dimension=0, tiled=True
    ).astype(jnp.float32)
    embed_own = lax.all_to_all(embed_cols, "mp", split_axis=0, concat_axis=1, tiled=True)
    decoder_in = jnp.concatenate([embed_own, text_embeds], axis=0)
    input_grad = norm_back(decoder_in, norm_grad, norm_gain)
    own_live = lax.dynamic_slice_in_dim(live_group, member * image_rows, image_rows, 0)
    image_own = jnp.where(own_live, input_grad[:image_rows], 0.0).astype(jnp.bfloat16)
    image_cols = lax.all_to_all(image_own, "mp", split_axis=1, concat_axis=0, tiled=True)
    text_grad = input_grad[image_rows:].astype(jnp.bfloat16)
    grad_scale = 1.0 / jnp.sqrt(jnp.float32(shards * groups * image_rows))
    proj_part = (
        lax.dot_general(
            vision_rows, image_cols, (((0,), (0,)), ((), ())), preferred_element_type=jnp.float32
        )
        * grad_scale
    )
    stored_rows = proj_flat.shape[0]
    padded = jnp.pad(proj_part.reshape(-1), (0, shards * stored_rows * 128 - used_count))
    padded = padded.reshape(shards * stored_rows, 128)
    proj_grad = summed_rows(padded, DP, (2, 1, 0), 0)
    return (text_grad, proj_grad)


def solution(mesh):
    finer = Mesh(mesh.devices.reshape(12, 4, 2, mesh.shape["mp"]), ("dp_0", "dp_1", "dp_2", "mp"))
    placed = (P(DP, None), P(DP), P(DP_MP, None), P(DP_MP, None), P(), P(None, "mp"), P(DP, "mp"))
    return jax.shard_map(
        body,
        mesh=finer,
        in_specs=placed,
        out_specs=(P(DP_MP, None), P(DP_MP, None)),
        check_vma=False,
    )
```

profile of v0, /device:TPU:2, one launch (start us, length us, event | category | flops | bytes accessed | tf_op | source)
XLA Modules:
  0.0 299.2 jit_solution(3021089597602194798)
XLA Ops:
  8.0 0.0 copy-start
  8.0 0.0 all-gather.2.cloned.1.call-start
  8.1 0.7 all-gather.2.cloned.1.call-update
  8.7 0.0 reduce-scatter.5.cloned.1.call-start
  8.8 0.4 copy-done
  9.2 8.9 %convolution_convert_fusion = bf16[1024,4096]{1,0:T(8,128)(2,1)} fusion(bf16[1024,512]{1,0:T(8,128)(2,1)S(1)} %copy-done, bf16[4096,512]{1,0:T(8,128)(2,1)} %param.12), kind=kOutput, calls=%fused_computation | convolution fusion | flops 4299161600 | bytes 13631488 | tf_op jit(solution)/shard_map/dot_general | solution.py:38
  18.2 0.0 reduce-scatter.5.cloned.1.call-update
  18.2 116.7 %all-gather.2.cloned.1.call-done = bf16[4608,128]{1,0:T(8,128)(2,1)} async-done(((bf16[48,128]{1,0:T(8,128)(2,1)}), bf16[4608,128]{1,0:T(8,128)(2,1)}) %all-gather.2.cloned.1.call-update) | async-done | bytes 1179664 | tf_op jit(solution)/shard_map/all_gather | solution.py:59
  134.8 0.0 slice-start
  134.8 1.2 slice-done
  136.1 0.0 copy-start.7
  136.1 0.6 reshape.57
  136.7 0.0 copy-start.4
  136.7 2.3 convolution_convert_fusion.1
  139.0 6.7 %all-to-all-start = ((bf16[8,32,512]{2,1,0:T(8,128)(2,1)}), bf16[8,32,512]{2,1,0:T(8,128)(2,1)S(1)}, u32[]{:S(2)}, u32[]{:S(2)}) async-start(bf16[8,32,512]{2,1,0:T(8,128)(2,1)} %bitcast), calls=%async_computation | async-start | bytes 524288 | tf_op jit(solution)/shard_map/all_to_all | solution.py:73
  145.7 0.0 reduce-scatter.7.cloned.1.call-start
  145.8 0.0 copy-done.7
  145.8 0.1 select_reduce_fusion
  145.9 0.1 dynamic-slice.3
  146.0 12.0 %all-to-all-done = bf16[8,32,512]{2,1,0:T(8,128)(2,1)S(1)} async-done(((bf16[8,32,512]{2,1,0:T(8,128)(2,1)}), bf16[8,32,512]{2,1,0:T(8,128)(2,1)S(1)}, u32[]{:S(2)}, u32[]{:S(2)}) %all-to-all-start) | async-done | bytes 262176 | tf_op jit(solution)/shard_map/all_to_all | solution.py:73
  158.0 0.0 reduce-scatter.5.cloned.1.call-done
  158.1 0.0 copy-start.3
  158.1 0.0 copy-done.6
  158.1 0.0 copy-done.4
  158.1 1.9 fusion
  160.0 0.0 copy-done.3
  160.0 0.0 copy-start.5
  160.0 0.7 fusion.2
  160.7 0.0 copy-start.1
  160.8 0.1 fusion.4
  160.9 14.1 %all_to_all.38 = bf16[32,8,512]{2,0,1:T(8,128)(2,1)S(1)} all-to-all(bf16[32,8,512]{2,0,1:T(8,128)(2,1)S(1)} %bitcast.34), channel_id=1, replica_groups=mesh['dp_0'=12,'dp_1'=4,'dp_2'=2,'mp'=8] {'mp'}, dimensions={1} | all-to-all | bytes 524288 | tf_op jit(solution)/shard_map/all_to_all | solution.py:78
  175.0 0.0 copy-done.1
  175.0 0.0 copy-done.5
  175.0 0.5 multiply_bitcast_fusion
  175.5 1.9 copy.19
  177.4 2.1 copy.23
  179.5 0.2 pad.4
  179.6 1.6 copy.20
  181.3 0.0 reduce-scatter.7.cloned.1.call-update
  181.3 0.0 reduce-scatter.9.cloned.1.call-start
  181.3 13.2 %reduce-scatter.7.cloned.1.call-done = f32[48,48,128]{2,1,0:T(8,128)} async-done(((f32[96,48,128]{2,1,0:T(8,128)}), f32[48,48,128]{2,1,0:T(8,128)}) %reduce-scatter.7.cloned.1.call-update) | async-done | bytes 1179664 | tf_op jit(solution)/shard_map/reduce_scatter | solution.py:22
  194.6 0.0 reduce-scatter.9.cloned.1.call-update
  194.6 0.0 reduce-scatter.11.cloned.1.call-start
  194.7 35.4 %reduce-scatter.9.cloned.1.call-done = f32[12,48,128]{2,1,0:T(8,128)} async-done(((f32[48,48,128]{2,1,0:T(8,128)}), f32[12,48,128]{2,1,0:T(8,128)}) %reduce-scatter.9.cloned.1.call-update) | async-done | bytes 294928 | tf_op jit(solution)/shard_map/reduce_scatter | solution.py:22
  230.0 0.0 reduce-scatter.11.cloned.1.call-update
  230.1 0.0 copy-done.2
  230.1 0.9 slice.21
  231.0 61.1 %reduce-scatter.11.cloned.1.call-done = f32[1,48,128]{2,1,0:T(8,128)} async-done(((f32[12,48,128]{2,1,0:T(8,128)}), f32[1,48,128]{2,1,0:T(8,128)}) %reduce-scatter.11.cloned.1.call-update) | async-done | bytes 24592 | tf_op jit(solution)/shard_map/reduce_scatter | solution.py:22
  (7 shorter events, 0.1 us)
Async XLA Ops:
  8.0 1.2 copy-start
  8.0 126.8 %all-gather.2.cloned.1.call-start = ((), (), s32[]{:S(2)}) async-start(), calls=%async_computation.6 | async-start | bytes 1191936 | tf_op jit(solution)/shard_map/all_gather | solution.py:59
  8.7 149.3 %reduce-scatter.5.cloned.1.call-start = ((), (), s32[]{:S(2)}) async-start(), calls=%async_computation.7 | async-start | bytes 9437184 | tf_op jit(solution)/shard_map/reduce_scatter | solution.py:70
  134.8 1.2 slice-start
  136.1 9.7 %copy-start.7 = (s32[8]{0:T(128)S(1)}, s32[8]{0:T(128)}, u32[]{:S(2)}) copy-start(s32[8]{0:T(128)} %param.8) | copy-start | bytes 100
  136.1 22.0 %copy-start.6 = (f32[4096]{0:T(1024)S(1)}, f32[4096]{0:T(1024)}, u32[]{:S(2)}) copy-start(f32[4096]{0:T(1024)} %param.11) | copy-start | bytes 49156
  136.7 21.3 %copy-start.4 = (bf16[96,4096]{1,0:T(8,128)(2,1)S(1)}, bf16[96,4096]{1,0:T(8,128)(2,1)}, u32[]{:S(2)}) copy-start(bf16[96,4096]{1,0:T(8,128)(2,1)} %param.10) | copy-start | bytes 2359300
  139.0 19.0 %all-to-all-start = ((bf16[8,32,512]{2,1,0:T(8,128)(2,1)}), bf16[8,32,512]{2,1,0:T(8,128)(2,1)S(1)}, u32[]{:S(2)}, u32[]{:S(2)}) async-start(bf16[8,32,512]{2,1,0:T(8,128)(2,1)} %bitcast), calls=%async_computation | async-start | bytes 524288 | tf_op jit(solution)/shard_map/all_to_all | solution.py:73
  145.7 48.8 %reduce-scatter.7.cloned.1.call-start = ((), (), s32[]{:S(2)}) async-start(), calls=%async_computation.8 | async-start | bytes 3538944 | tf_op jit(solution)/shard_map/reduce_scatter | solution.py:22
  158.1 1.9 copy-start.3
  160.0 15.0 %copy-start.5 = (bf16[256,1024]{1,0:T(8,128)(2,1)S(1)}, bf16[256,1024]{1,0:T(8,128)(2,1)}, u32[]{:S(2)}) copy-start(bf16[256,1024]{1,0:T(8,128)(2,1)} %param.7) | copy-start | bytes 1572868
  160.7 14.3 %copy-start.1 = (bf16[128,4096]{1,0:T(8,128)(2,1)}, bf16[128,4096]{1,0:T(8,128)(2,1)S(1)}, u32[]{:S(2)}) copy-start(bf16[128,4096]{1,0:T(8,128)(2,1)S(1)} %fusion.2) | copy-start | bytes 3145732
  181.3 48.8 %copy-start.2 = (bf16[128,4096]{1,0:T(8,128)(2,1)S(1)}, bf16[128,4096]{1,0:T(8,128)(2,1)}, u32[]{:S(2)}) copy-start(bf16[128,4096]{1,0:T(8,128)(2,1)} %copy-done.1) | copy-start | bytes 3145732
  181.3 48.7 %reduce-scatter.9.cloned.1.call-start = ((), (), s32[]{:S(2)}) async-start(), calls=%async_computation.9 | async-start | bytes 1474560 | tf_op jit(solution)/shard_map/reduce_scatter | solution.py:22
  194.6 97.5 %reduce-scatter.11.cloned.1.call-start = ((), (), s32[]{:S(2)}) async-start(), calls=%async_computation.10 | async-start | bytes 319488 | tf_op jit(solution)/shard_map/reduce_scatter | solution.py:22
Sparse Core Ops, SparseCore 0:
  12.5 122.2 all-gather.1
  181.4 13.1 reduce-scatter.6
  197.7 32.2 reduce-scatter.8
  233.6 58.4 reduce-scatter.10
Sparse Core Ops, SparseCore 1:
  18.3 106.6 reduce-scatter.4
where the time goes:
time: 300 us; the launch traced here: 299 us
  waiting for transfers between devices  239 us (80%)
  between operations  15.4 us (5%)
  blocking collectives  14.1 us (5%)
  matrix products  11.6 us (4%)
  local copies, waits for them, and re-layouts  9.17 us (3%)
  starting transfers between devices  6.94 us (2%)
    all_gather x1, waiting for transfers between devices, body(): gathered = lax.all_gather(proj_flat, DP, axis=0, tiled=True)  117 us
    reduce_scatter x3, waiting for transfers between devices, own_block(): blocks = lax.psum_scatter(blocks, axes[k], scatter_dimension=0, tiled=True)  110 us
    all_to_all x1, blocking collectives, body(): lax.all_to_all(image_own, 'mp', split_axis=1, concat_axis=0, tiled=True)  14.1 us
    all_to_all x1, waiting for transfers between devices, body(): lax.all_to_all(embed_cols, 'mp', split_axis=0, concat_axis=1, tiled=True)  12 us
    dot_general x1, matrix products, row_term(): lax.dot_general(left, weight, (((1,), (1,)), ((), ())), preferred_element...  8.93 us
    all_to_all x1, starting transfers between devices, body(): lax.all_to_all(embed_cols, 'mp', split_axis=0, concat_axis=1, tiled=True)  6.74 us
  transfers between devices with their start and end apart: 6, of which 5 were waited for; matrix products, arithmetic and copies ran while one was open for 4% of the time, Pallas kernels for 0%

commit v1 on v0

v1 whole, which is shorter than its diff:
```python
import jax
import jax.numpy as jnp
from jax import lax
from jax.sharding import Mesh
from jax.sharding import PartitionSpec as P

IMG_MAX = 4
PATCH = 8
DP = ("z", "x", "c")
DP_MP = ("z", "x", "c", "y")

norm_eps = 1e-05


def spread(block, axis):
    n = lax.axis_size(axis)
    copies = jnp.broadcast_to(block[None], (n, *block.shape))
    return lax.all_to_all(copies, axis, split_axis=0, concat_axis=0, tiled=True)


def summed(blocks, axis):
    parts = lax.all_to_all(
        blocks.astype(jnp.bfloat16), axis, split_axis=0, concat_axis=0, tiled=True
    )
    return jnp.sum(parts.astype(jnp.float32), axis=0)


def contract_last(left, right):
    return lax.dot_general(
        left, right, (((1,), (1,)), ((), ())), preferred_element_type=jnp.float32
    )


def body(vision_rows, image_count, proj_flat, text_embeds, norm_gain, q_weight, q_grad):
    groups = lax.axis_size("y")
    nz, nx, nc = (lax.axis_size(a) for a in DP)
    shards = nz * nx * nc
    enc_width = vision_rows.shape[1]
    block_cols = q_weight.shape[1]
    width = q_weight.shape[0]
    image_rows = IMG_MAX * PATCH
    own_rows = q_grad.shape[0] // groups
    text_rows = own_rows - image_rows
    per_shard = proj_flat.shape[0] * 128 // block_cols
    bf16 = jnp.bfloat16

    q_own = q_grad.reshape(groups, own_rows, block_cols)
    q_image = q_own[:, :image_rows].reshape(groups * image_rows, block_cols)
    q_text = q_own[:, image_rows:].reshape(groups * text_rows, block_cols)
    image_part = contract_last(q_weight, q_image).astype(bf16)
    image_norm = lax.psum_scatter(image_part, "y", scatter_dimension=0, tiled=True)
    text_part = contract_last(q_text, q_weight).astype(bf16)
    text_norm = lax.psum_scatter(text_part, "y", scatter_dimension=0, tiled=True)

    order = jnp.arange(shards * per_shard, dtype=jnp.int32)
    row = order % per_shard
    zi = order // per_shard % nz
    xi = order // (per_shard * nz) % nx
    ci = order // (per_shard * nz * nx)
    source = ((zi * nx + xi) * nc + ci) * per_shard + row
    pick = (jnp.arange(enc_width, dtype=jnp.int32)[:, None] == source[None, :]).astype(bf16)
    vision = jnp.dot(vision_rows, pick, preferred_element_type=jnp.float32).astype(bf16)

    shard = proj_flat.reshape(per_shard, block_cols)
    over_z = spread(shard, "z").reshape(nz * per_shard, block_cols)
    over_x = spread(over_z, "x").reshape(nx * nz * per_shard, block_cols)
    proj = spread(over_x, "c").reshape(shards * per_shard, block_cols)
    embed = lax.dot_general(
        proj, vision, (((0,), (1,)), ((), ())), preferred_element_type=jnp.float32
    ).astype(bf16)

    gain_own = lax.dynamic_slice_in_dim(norm_gain, lax.axis_index("y") * block_cols, block_cols, 0)
    inputs = embed.astype(jnp.float32)
    scaled = gain_own[:, None] * image_norm.astype(jnp.float32)
    stats = jnp.stack([jnp.sum(inputs * inputs, axis=0), jnp.sum(scaled * inputs, axis=0)])
    stats = jnp.sum(spread(stats, "y").reshape(groups, 2, groups * image_rows), axis=0) / width
    inv_rms = lax.rsqrt(stats[0] + norm_eps)
    row_ids = jnp.arange(groups * image_rows, dtype=jnp.int32)
    owner_match = (row_ids // image_rows)[:, None] == jnp.arange(groups, dtype=jnp.int32)[None, :]
    counts = jnp.sum(jnp.where(owner_match, image_count[None, :], 0), axis=1)
    live = row_ids % image_rows // PATCH < counts
    image_grad = inv_rms[None, :] * scaled - inputs * (inv_rms**3 * stats[1])[None, :]
    image_grad = jnp.where(live[None, :], image_grad, 0.0).astype(bf16)
    grad_scale = 1.0 / jnp.sqrt(jnp.float32(shards * groups * image_rows))
    proj_part = (
        lax.dot_general(
            vision, image_grad, (((0,), (1,)), ((), ())), preferred_element_type=jnp.float32
        )
        * grad_scale
    )
    part = summed(proj_part.reshape(nc, nx * nz * per_shard, block_cols), "c")
    part = summed(part.reshape(nx, nz * per_shard, block_cols), "x")
    part = summed(part.reshape(nz, per_shard, block_cols), "z")
    proj_grad = part.reshape(proj_flat.shape)

    text_in = text_embeds.astype(jnp.float32)
    text_rms = lax.rsqrt(jnp.mean(text_in * text_in, axis=-1, keepdims=True) + norm_eps)
    text_scaled = norm_gain[None, :] * text_norm.astype(jnp.float32)
    inner = jnp.mean(text_scaled * text_in, axis=-1, keepdims=True)
    text_grad = (text_rms * text_scaled - text_in * text_rms**3 * inner).astype(bf16)
    return (text_grad, proj_grad)


def solution(mesh):
    finer = Mesh(mesh.devices.reshape(12, 4, 2, mesh.shape["mp"]), DP_MP)
    placed = (P(DP, None), P(DP), P(DP_MP, None), P(DP_MP, None), P(), P(None, "y"), P(DP, "y"))
    return jax.shard_map(
        body,
        mesh=finer,
        in_specs=placed,
        out_specs=(P(DP_MP, None), P(DP_MP, None)),
        check_vma=False,
    )
```

time: 300 us -> 162 us (0.54)
  the two profiles are of different devices: /device:TPU:2 before, /device:TPU:1 now
where the time goes in v1:
time: 162 us; the launch traced here: 161 us
  waiting for transfers between devices  51.6 us (32%)
  blocking collectives  42.9 us (26%)
  starting transfers between devices  26.6 us (16%)
  matrix products  15.7 us (10%)
  between operations  14.2 us (9%)
  local copies, waits for them, and re-layouts  5.96 us (4%)
  other arithmetic  3.87 us (2%)
    all_to_all x3, blocking collectives, summed(): lax.all_to_all(blocks.astype(jnp.bfloat16), axis, split_axis=0, concat_ax...  34.7 us
    all_to_all x3, starting transfers between devices, spread(): return lax.all_to_all(copies, axis, split_axis=0, concat_axis=0, tiled=True)  26.5 us
    reduce_scatter x1, waiting for transfers between devices, body(): lax.psum_scatter(text_part, 'y', scatter_dimension=0, tiled=True)  26.2 us
    all_to_all x3, waiting for transfers between devices, spread(): return lax.all_to_all(copies, axis, split_axis=0, concat_axis=0, tiled=True)  25.3 us
    dot_general x2, matrix products, contract_last(): lax.dot_general(left, right, (((1,), (1,)), ((), ())), preferred_element_...  12.6 us
    all_to_all x1, blocking collectives, spread(): return lax.all_to_all(copies, axis, split_axis=0, concat_axis=0, tiled=True)  8.2 us
  transfers between devices with their start and end apart: 5, of which 4 were waited for; matrix products, arithmetic and copies ran while one was open for 9% of the time, Pallas kernels for 0%

profile of v1, /device:TPU:1, one launch (start us, length us, event | category | flops | bytes accessed | tf_op | source)
XLA Modules:
  0.0 160.8 jit_solution(1649555161163932665)
XLA Ops:
  7.2 0.0 copy-start
  7.2 0.0 reduce-scatter.5.cloned.1.call-start
  7.2 1.0 slice.17
  8.3 4.8 %convolution_convert_fusion.1 = bf16[4096,256]{0,1:T(8,128)(2,1)} fusion(bf16[4096,512]{1,0:T(8,128)(2,1)} %param.12, bf16[256,512]{1,0:T(8,128)(2,1)S(1)} %bitcast.28), kind=kOutput, calls=%fused_computation.1 | convolution fusion | flops 1074790400 | bytes 6553600 | tf_op jit(solution)/shard_map/dot_general | solution.py:29
  13.1 0.0 copy-start.3
  13.1 0.0 reduce-scatter.5.cloned.1.call-update
  13.1 0.0 reduce-scatter.3.cloned.1.call-start
  13.1 1.1 copy-done.3
  14.3 0.1 slice.16
  14.4 7.8 %convolution_convert_fusion = bf16[768,4096]{1,0:T(8,128)(2,1)} fusion(bf16[768,512]{1,0:T(8,128)(2,1)S(1)} %bitcast.27, bf16[4096,512]{1,0:T(8,128)(2,1)} %param.12), kind=kOutput, calls=%fused_computation | convolution fusion | flops 3224371200 | bytes 11272192 | tf_op jit(solution)/shard_map/dot_general | solution.py:29
  22.2 0.0 copy-start.5
  22.2 0.0 copy-start.4
  22.2 0.0 reduce-scatter.3.cloned.1.call-update
  22.2 0.7 copy-done.5
  22.9 0.0 copy-start.6
  22.9 0.7 broadcast_in_dim.67
  23.6 15.7 %all-to-all-start = ((bf16[12,12,512]{2,1,0:T(8,128)(2,1)}), bf16[12,12,512]{2,1,0:T(8,128)(2,1)S(1)}, u32[]{:S(2)}, u32[]{:S(2)}) async-start(bf16[12,12,512]{2,1,0:T(8,128)(2,1)} %broadcast_in_dim.67), calls=%async_computation.1 | async-start | bytes 393216 | tf_op jit(solution)/shard_map/all_to_all | solution.py:18
  39.3 0.0 copy-done.4
  39.3 0.1 dynamic_slice.3
  39.4 12.3 %all-to-all-done = bf16[12,12,512]{2,1,0:T(8,128)(2,1)S(1)} async-done(((bf16[12,12,512]{2,1,0:T(8,128)(2,1)}), bf16[12,12,512]{2,1,0:T(8,128)(2,1)S(1)}, u32[]{:S(2)}, u32[]{:S(2)}) %all-to-all-start) | async-done | bytes 147488 | tf_op jit(solution)/shard_map/all_to_all | solution.py:18
  51.8 0.9 broadcast_in_dim.69
  52.6 4.0 %all-to-all-start.1 = ((bf16[4,144,512]{2,1,0:T(8,128)(2,1)}), bf16[4,144,512]{2,1,0:T(8,128)(2,1)S(1)}, u32[]{:S(2)}, u32[]{:S(2)}) async-start(bf16[4,144,512]{2,1,0:T(8,128)(2,1)} %broadcast_in_dim.69), calls=%async_computation.2 | async-start | bytes 1179648 | tf_op jit(solution)/shard_map/all_to_all | solution.py:18
  56.6 0.0 copy-done.6
  56.6 0.1 select_reduce_fusion
  56.7 0.0 copy-done
  56.7 0.8 convolution_convert_fusion.2
  57.6 6.4 %all-to-all-done.1 = bf16[4,144,512]{2,1,0:T(8,128)(2,1)S(1)} async-done(((bf16[4,144,512]{2,1,0:T(8,128)(2,1)}), bf16[4,144,512]{2,1,0:T(8,128)(2,1)S(1)}, u32[]{:S(2)}, u32[]{:S(2)}) %all-to-all-start.1) | async-done | bytes 589856 | tf_op jit(solution)/shard_map/all_to_all | solution.py:18
  63.9 0.1 broadcast_in_dim.71
  64.0 8.2 %all_to_all.35 = bf16[2,576,512]{2,1,0:T(8,128)(2,1)S(1)} all-to-all(bf16[2,576,512]{2,1,0:T(8,128)(2,1)S(1)} %broadcast_in_dim.71), channel_id=1, replica_groups=mesh['z'=12,'x'=4,'c'=2,'y'=8] {'c'}, dimensions={0} | all-to-all | bytes 2359296 | tf_op jit(solution)/shard_map/all_to_all | solution.py:18
  72.2 0.0 reduce-scatter.5.cloned.1.call-done
  72.2 1.7 %multiply_reduce_fusion.1 = (f32[256]{0:T(256)S(1)}, f32[256]{0:T(256)S(1)}, f32[512,256]{0,1:T(8,128)S(1)}) fusion(bf16[512,256]{0,1:T(8,128)(2,1)} %reduce-scatter.5.cloned.1.call-done, f32[512]{0:T(512)S(1)} %dynamic_slice.3, bf16[1152,256]{1,0:T(8,128)(2,1)S(1)} %convolution_convert_fusion.2, bf16[1152,512]{1,0:T(8,128)(2,1)S(1)} %bitcast.23), kind=kOutput, calls=%fused_computation.23 | convolution fusion | flops 303037952 | bytes 2560000 | tf_op jit(solution)/shard_map/dot_general | solution.py:68
  73.9 0.6 broadcast_in_dim.72
  74.5 6.8 %all-to-all-start.3 = ((f32[8,2,256]{2,1,0:T(2,128)}), f32[8,2,256]{2,1,0:T(2,128)S(1)}, u32[]{:S(2)}, u32[]{:S(2)}) async-start(f32[8,2,256]{2,1,0:T(2,128)} %broadcast_in_dim.72), calls=%async_computation.5 | async-start | bytes 32768 | tf_op jit(solution)/shard_map/all_to_all | solution.py:18
  81.4 6.6 %all-to-all-done.3 = f32[8,2,256]{2,1,0:T(2,128)S(1)} async-done(((f32[8,2,256]{2,1,0:T(2,128)}), f32[8,2,256]{2,1,0:T(2,128)S(1)}, u32[]{:S(2)}, u32[]{:S(2)}) %all-to-all-start.3) | async-done | bytes 16416 | tf_op jit(solution)/shard_map/all_to_all | solution.py:18
  88.0 0.0 copy-done.7
  88.0 0.6 fusion.1
  88.6 6.1 %all_to_all.36 = bf16[2,576,512]{2,1,0:T(8,128)(2,1)S(1)} all-to-all(bf16[2,576,512]{2,1,0:T(8,128)(2,1)S(1)} %bitcast.24), channel_id=1, replica_groups=mesh['z'=12,'x'=4,'c'=2,'y'=8] {'c'}, dimensions={0} | all-to-all | bytes 2359296 | tf_op jit(solution)/shard_map/all_to_all | solution.py:22
  94.7 0.6 reduce_sum.93
  95.3 0.0 copy-start.1
  95.3 12.1 %all_to_all.37 = bf16[4,144,512]{2,1,0:T(8,128)(2,1)S(1)} all-to-all(bf16[4,144,512]{2,1,0:T(8,128)(2,1)S(1)} %bitcast.22), channel_id=1, replica_groups=mesh['z'=12,'x'=4,'c'=2,'y'=8] {'x'}, dimensions={0} | all-to-all | bytes 1179648 | tf_op jit(solution)/shard_map/all_to_all | solution.py:22
  107.4 0.1 reduce_sum.94
  107.6 16.5 %all_to_all.38 = bf16[12,12,512]{2,1,0:T(8,128)(2,1)S(1)} all-to-all(bf16[12,12,512]{2,1,0:T(8,128)(2,1)S(1)} %convert_element_type.69), channel_id=1, replica_groups=mesh['z'=12,'x'=4,'c'=2,'y'=8] {'z'}, dimensions={0} | all-to-all | bytes 294912 | tf_op jit(solution)/shard_map/all_to_all | solution.py:22
  124.1 0.6 reshape.150
  124.7 26.2 %reduce-scatter.3.cloned.1.call-done = bf16[96,4096]{1,0:T(8,128)(2,1)} async-done(((bf16[768,4096]{1,0:T(8,128)(2,1)}), bf16[96,4096]{1,0:T(8,128)(2,1)}) %reduce-scatter.3.cloned.1.call-update) | async-done | bytes 786448 | tf_op jit(solution)/shard_map/reduce_scatter | solution.py:53
  150.9 0.0 copy-done.1
  150.9 1.7 %fusion.4 = (f32[96]{0:T(128)S(1)}, f32[96]{0:T(128)S(1)}) fusion(bf16[96,4096]{1,0:T(8,128)(2,1)S(1)} %copy-done.1, bf16[96,4096]{1,0:T(8,128)(2,1)} %reduce-scatter.3.cloned.1.call-done, f32[4096]{0:T(1024)S(1)} %copy-done.4), kind=kLoop, calls=%fused_computation.11 | loop fusion | flops 2752320 | bytes 1590016 | tf_op jit(solution)/shard_map/reduce_sum | solution.py:97
  152.6 0.0 copy-done.2
  152.6 1.3 fusion.7
  (15 shorter events, 0.2 us)
Async XLA Ops:
  7.2 49.6 %copy-start = (bf16[256,1024]{1,0:T(8,128)(2,1)S(1)}, bf16[256,1024]{1,0:T(8,128)(2,1)}, u32[]{:S(2)}) copy-start(bf16[256,1024]{1,0:T(8,128)(2,1)} %param.7) | copy-start | bytes 1572868
  7.2 65.0 %reduce-scatter.5.cloned.1.call-start = ((), (), s32[]{:S(2)}) async-start(), calls=%async_computation.10 | async-start | bytes 2359296 | tf_op jit(solution)/shard_map/reduce_scatter | solution.py:51
  13.1 1.2 copy-start.3
  13.1 137.8 %reduce-scatter.3.cloned.1.call-start = ((), (), s32[]{:S(2)}) async-start(), calls=%async_computation.9 | async-start | bytes 7077888 | tf_op jit(solution)/shard_map/reduce_scatter | solution.py:53
  22.2 0.7 copy-start.5
  22.2 17.1 %copy-start.4 = (f32[4096]{0:T(1024)S(1)}, f32[4096]{0:T(1024)}, u32[]{:S(2)}) copy-start(f32[4096]{0:T(1024)} %param.11) | copy-start | bytes 49156
  22.9 33.8 %copy-start.6 = (s32[8]{0:T(128)S(1)}, s32[8]{0:T(128)}, u32[]{:S(2)}) copy-start(s32[8]{0:T(128)} %param.8) | copy-start | bytes 100
  23.6 28.1 %all-to-all-start = ((bf16[12,12,512]{2,1,0:T(8,128)(2,1)}), bf16[12,12,512]{2,1,0:T(8,128)(2,1)S(1)}, u32[]{:S(2)}, u32[]{:S(2)}) async-start(bf16[12,12,512]{2,1,0:T(8,128)(2,1)} %broadcast_in_dim.67), calls=%async_computation.1 | async-start | bytes 393216 | tf_op jit(solution)/shard_map/all_to_all | solution.py:18
  52.6 11.3 %all-to-all-start.1 = ((bf16[4,144,512]{2,1,0:T(8,128)(2,1)}), bf16[4,144,512]{2,1,0:T(8,128)(2,1)S(1)}, u32[]{:S(2)}, u32[]{:S(2)}) async-start(bf16[4,144,512]{2,1,0:T(8,128)(2,1)} %broadcast_in_dim.69), calls=%async_computation.2 | async-start | bytes 1179648 | tf_op jit(solution)/shard_map/all_to_all | solution.py:18
  72.2 15.8 %copy-start.7 = (bf16[512,256]{0,1:T(8,128)(2,1)S(1)}, bf16[512,256]{0,1:T(8,128)(2,1)}, u32[]{:S(2)}) copy-start(bf16[512,256]{0,1:T(8,128)(2,1)} %reduce-scatter.5.cloned.1.call-done) | copy-start | bytes 786436
  74.5 13.4 %all-to-all-start.3 = ((f32[8,2,256]{2,1,0:T(2,128)}), f32[8,2,256]{2,1,0:T(2,128)S(1)}, u32[]{:S(2)}, u32[]{:S(2)}) async-start(f32[8,2,256]{2,1,0:T(2,128)} %broadcast_in_dim.72), calls=%async_computation.5 | async-start | bytes 32768 | tf_op jit(solution)/shard_map/all_to_all | solution.py:18
  95.3 55.6 %copy-start.1 = (bf16[96,4096]{1,0:T(8,128)(2,1)S(1)}, bf16[96,4096]{1,0:T(8,128)(2,1)}, u32[]{:S(2)}) copy-start(bf16[96,4096]{1,0:T(8,128)(2,1)} %param.10) | copy-start | bytes 2359300
  150.9 1.7 %copy-start.2 = (bf16[96,4096]{1,0:T(8,128)(2,1)S(1)}, bf16[96,4096]{1,0:T(8,128)(2,1)}, u32[]{:S(2)}) copy-start(bf16[96,4096]{1,0:T(8,128)(2,1)} %reduce-scatter.3.cloned.1.call-done) | copy-start | bytes 2359300
Sparse Core Ops, SparseCore 0:
  13.2 50.9 reduce-scatter.4
  67.4 83.5 reduce-scatter.2

commit v2 on v1

v2 whole, which is shorter than its diff:
```python
import jax
import jax.numpy as jnp
from jax import lax
from jax.sharding import Mesh
from jax.sharding import PartitionSpec as P

IMG_MAX = 4
PATCH = 8
DP = ("z", "x", "c")
DP_MP = ("z", "x", "c", "y")

norm_eps = 1e-05
bf16 = jnp.bfloat16
f32 = jnp.float32


def dot(left, right, dims):
    return lax.dot_general(left, right, (dims, ((), ())), preferred_element_type=f32)


def spread(block, axis):
    n = lax.axis_size(axis)
    copies = jnp.broadcast_to(block[None], (n, *block.shape))
    return lax.all_to_all(copies, axis, split_axis=0, concat_axis=0, tiled=True)


def summed(blocks, axis):
    parts = lax.all_to_all(blocks.astype(bf16), axis, split_axis=0, concat_axis=0, tiled=True)
    return jnp.sum(parts.astype(f32), axis=0)


def gathered(shard):
    for axis in ("z", "x", "c"):
        parts = spread(shard, axis)
        shard = parts.reshape(-1, shard.shape[-1])
    return shard


def body(vision_rows, image_count, proj_flat, text_embeds, norm_gain, q_weight, q_grad):
    groups = lax.axis_size("y")
    member = lax.axis_index("y")
    nz, nx, nc = (lax.axis_size(a) for a in DP)
    shards = nz * nx * nc
    enc = vision_rows.shape[1]
    cols = q_weight.shape[1]
    width = q_weight.shape[0]
    image_rows = IMG_MAX * PATCH
    own_rows = q_grad.shape[0] // groups
    text_rows = own_rows - image_rows
    per_shard = proj_flat.shape[0] * 128 // cols
    enc_block = enc // groups

    q_own = q_grad.reshape(groups, own_rows, cols)
    q_text = q_own[:, image_rows:].reshape(groups * text_rows, cols)
    text_part = dot(q_text, q_weight, ((1,), (1,))).astype(bf16)
    text_norm = lax.psum_scatter(text_part, "y", scatter_dimension=0, tiled=True)

    shard = proj_flat.reshape(per_shard, cols)
    gain_blocks = norm_gain.reshape(groups, 1, cols)
    group_rows = (spread(shard, "y").astype(f32) * gain_blocks).astype(bf16)
    through = dot(group_rows, q_weight.reshape(groups, cols, cols), ((0, 2), (0, 1))).astype(bf16)
    proj = gathered(shard)
    through = gathered(through)

    order = jnp.arange(shards * per_shard, dtype=jnp.int32)
    row = order % per_shard
    zi = order // per_shard % nz
    xi = order // (per_shard * nz) % nx
    ci = order // (per_shard * nz * nx)
    source = ((zi * nx + xi) * nc + ci) * per_shard + row
    pick = (jnp.arange(enc, dtype=jnp.int32)[:, None] == source[None, :]).astype(bf16)
    vision = dot(vision_rows, pick, ((1,), (0,))).astype(bf16)
    proj_rows = dot(pick, proj, ((1,), (0,))).astype(bf16)

    q_image = q_own[:, :image_rows].reshape(groups * image_rows, cols).T.astype(f32)
    embed = dot(proj, vision, ((0,), (1,)))
    pulled = dot(through, vision, ((0,), (1,)))
    stats = jnp.stack([jnp.sum(embed * embed, axis=0), jnp.sum(q_image * pulled, axis=0)])
    stats = jnp.sum(spread(stats, "y"), axis=0) / width
    inv_rms = lax.rsqrt(stats[0] + norm_eps)
    row_ids = jnp.arange(groups * image_rows, dtype=jnp.int32)
    owner_match = (row_ids // image_rows)[:, None] == jnp.arange(groups, dtype=jnp.int32)[None, :]
    counts = jnp.sum(jnp.where(owner_match, image_count[None, :], 0), axis=1)
    live = row_ids % image_rows // PATCH < counts
    grad_scale = 1.0 / jnp.sqrt(f32(shards * groups * image_rows))
    first = jnp.where(live, inv_rms, 0.0) * grad_scale
    second = jnp.where(live, inv_rms**3 * stats[1], 0.0) * grad_scale

    vision_block = lax.dynamic_slice_in_dim(vision_rows, member * enc_block, enc_block, 1)
    right = jnp.concatenate(
        [
            (q_image * first[None, :]).astype(bf16),
            (vision_block.T.astype(f32) * second[None, :]).astype(bf16),
        ],
        axis=0,
    )
    part = dot(vision, right, ((0,), (1,)))
    part = summed(part.reshape(nc, nx * nz * per_shard, cols + enc_block), "c")
    part = summed(part.reshape(nx, nz * per_shard, cols + enc_block), "x")
    part = summed(part.reshape(nz, per_shard, cols + enc_block), "z").astype(bf16)
    through_weight = dot(part[:, :cols], q_weight, ((1,), (1,))).astype(bf16)
    through_weight = through_weight.reshape(per_shard, groups, cols).transpose(1, 0, 2)
    moments = jnp.broadcast_to(part[None, :, cols:], (groups, per_shard, enc_block))
    parts = lax.all_to_all(
        jnp.concatenate([through_weight, moments], axis=2), "y", split_axis=0, concat_axis=0, tiled=True
    )
    gain_own = lax.dynamic_slice_in_dim(norm_gain, member * cols, cols, 0)
    plain = jnp.sum(parts[:, :, :cols].astype(f32), axis=0) * gain_own[None, :]
    radial = dot(parts[:, :, cols:], proj_rows.reshape(groups, enc_block, cols), ((0, 2), (0, 1)))
    proj_grad = (plain - radial).reshape(proj_flat.shape)

    text_in = text_embeds.astype(f32)
    text_rms = lax.rsqrt(jnp.mean(text_in * text_in, axis=-1, keepdims=True) + norm_eps)
    text_scaled = norm_gain[None, :] * text_norm.astype(f32)
    inner = jnp.mean(text_scaled * text_in, axis=-1, keepdims=True)
    text_grad = (text_rms * text_scaled - text_in * text_rms**3 * inner).astype(bf16)
    return (text_grad, proj_grad)


def solution(mesh):
    finer = Mesh(mesh.devices.reshape(12, 4, 2, mesh.shape["mp"]), DP_MP)
    placed = (P(DP, None), P(DP), P(DP_MP, None), P(DP_MP, None), P(), P(None, "y"), P(DP, "y"))
    return jax.shard_map(
        body,
        mesh=finer,
        in_specs=placed,
        out_specs=(P(DP_MP, None), P(DP_MP, None)),
        check_vma=False,
    )
```

time: 162 us -> 199 us (1.23)
  the two profiles are of different devices: /device:TPU:1 before, /device:TPU:2 now
where the time goes in v2:
time: 199 us; the launch traced here: 198 us
  waiting for transfers between devices  67.4 us (34%)
  blocking collectives  45 us (23%)
  starting transfers between devices  38.7 us (19%)
  matrix products  18.6 us (9%)
  between operations  14.4 us (7%)
  local copies, waits for them, and re-layouts  8.85 us (4%)
  other arithmetic  4.89 us (2%)
    all_to_all x5, waiting for transfers between devices, spread(): return lax.all_to_all(copies, axis, split_axis=0, concat_axis=0, tiled=True)  43.8 us
    all_to_all x5, starting transfers between devices, spread(): return lax.all_to_all(copies, axis, split_axis=0, concat_axis=0, tiled=True)  31.8 us
    all_to_all x3, blocking collectives, spread(): return lax.all_to_all(copies, axis, split_axis=0, concat_axis=0, tiled=True)  25.4 us
    all_to_all x2, blocking collectives, summed(): lax.all_to_all(blocks.astype(bf16), axis, split_axis=0, concat_axis=0, ti...  19.6 us
    dot_general x9, matrix products, dot(): lax.dot_general(left, right, (dims, ((), ())), preferred_element_type=f32)  18.6 us
    all_to_all x1, waiting for transfers between devices, summed(): lax.all_to_all(blocks.astype(bf16), axis, split_axis=0, concat_axis=0, ti...  15.8 us
    all_to_all x1, waiting for transfers between devices, body(): lax.all_to_all(jnp.concatenate([through_weight, moments], axis=2), 'y', s...  7.8 us
    broadcast_in_dim x11, local copies, waits for them, and re-layouts, spread(): copies = jnp.broadcast_to(block[None], (n, *block.shape))  4.03 us
  transfers between devices with their start and end apart: 8, of which 7 were waited for; matrix products, arithmetic and copies ran while one was open for 10% of the time, Pallas kernels for 0%

profile of v2, /device:TPU:2, one launch (start us, length us, event | category | flops | bytes accessed | tf_op | source)
XLA Modules:
  0.0 197.8 jit_solution(17445783794166396012)
XLA Ops:
  7.2 1.2 slice.32
  8.5 7.8 %convolution_convert_fusion = bf16[768,4096]{1,0:T(8,128)(2,1)} fusion(bf16[768,512]{1,0:T(8,128)(2,1)S(1)} %bitcast.62, bf16[4096,512]{1,0:T(8,128)(2,1)} %param.12), kind=kOutput, calls=%fused_computation | convolution fusion | flops 3224371200 | bytes 11272192 | tf_op jit(solution)/shard_map/dot_general | solution.py:18
  16.3 0.7 copy-done.6
  17.0 16.0 %all_to_all.60 = bf16[8,12,512]{2,1,0:T(8,128)(2,1)S(1)} all-to-all(bf16[8,12,512]{2,1,0:T(8,128)(2,1)S(1)} %broadcast_in_dim.94), channel_id=1, replica_groups=mesh['z'=12,'x'=4,'c'=2,'y'=8] {'y'}, dimensions={0} | all-to-all | bytes 196608 | tf_op jit(solution)/shard_map/all_to_all | solution.py:24
  33.0 0.7 broadcast_in_dim.48
  33.7 15.2 %all-to-all-start = ((bf16[12,12,512]{2,1,0:T(8,128)(2,1)}), bf16[12,12,512]{2,1,0:T(8,128)(2,1)S(1)}, u32[]{:S(2)}, u32[]{:S(2)}) async-start(bf16[12,12,512]{2,1,0:T(8,128)(2,1)} %broadcast_in_dim.48), calls=%async_computation.1 | async-start | bytes 393216 | tf_op jit(solution)/shard_map/all_to_all | solution.py:24
  48.9 2.8 %fusion.14 = bf16[12,512]{1,0:T(8,128)(2,1)S(1)} fusion(bf16[8,512,512]{2,1,0:T(8,128)(2,1)} %bitcast.51, bf16[8,12,512]{2,1,0:T(8,128)(2,1)S(1)} %all_to_all.60, f32[8,512]{1,0:T(8,128)S(1)} %mul.152), kind=kOutput, calls=%fused_computation.26 | convolution fusion | flops 50485248 | bytes 4321280 | tf_op jit(solution)/shard_map/dot_general | solution.py:18
  51.7 9.8 %all-to-all-done = bf16[12,12,512]{2,1,0:T(8,128)(2,1)S(1)} async-done(((bf16[12,12,512]{2,1,0:T(8,128)(2,1)}), bf16[12,12,512]{2,1,0:T(8,128)(2,1)S(1)}, u32[]{:S(2)}, u32[]{:S(2)}) %all-to-all-start) | async-done | bytes 147488 | tf_op jit(solution)/shard_map/all_to_all | solution.py:24
  61.6 0.7 broadcast_in_dim.95
  62.3 3.5 %all-to-all-start.4 = ((bf16[12,12,512]{2,1,0:T(8,128)(2,1)}), bf16[12,12,512]{2,1,0:T(8,128)(2,1)S(1)}, u32[]{:S(2)}, u32[]{:S(2)}) async-start(bf16[12,12,512]{2,1,0:T(8,128)(2,1)} %broadcast_in_dim.95), calls=%async_computation.5 | async-start | bytes 393216 | tf_op jit(solution)/shard_map/all_to_all | solution.py:24
  65.8 1.0 slice.33
  66.8 12.1 %all-to-all-done.4 = bf16[12,12,512]{2,1,0:T(8,128)(2,1)S(1)} async-done(((bf16[12,12,512]{2,1,0:T(8,128)(2,1)}), bf16[12,12,512]{2,1,0:T(8,128)(2,1)S(1)}, u32[]{:S(2)}, u32[]{:S(2)}) %all-to-all-start.4) | async-done | bytes 147488 | tf_op jit(solution)/shard_map/all_to_all | solution.py:24
  78.9 0.9 broadcast_in_dim.50
  79.8 4.8 %all-to-all-start.1 = ((bf16[4,144,512]{2,1,0:T(8,128)(2,1)}), bf16[4,144,512]{2,1,0:T(8,128)(2,1)S(1)}, u32[]{:S(2)}, u32[]{:S(2)}) async-start(bf16[4,144,512]{2,1,0:T(8,128)(2,1)} %broadcast_in_dim.50), calls=%async_computation.2 | async-start | bytes 1179648 | tf_op jit(solution)/shard_map/all_to_all | solution.py:24
  84.7 0.2 copy.18
  85.0 6.6 %all-to-all-done.1 = bf16[4,144,512]{2,1,0:T(8,128)(2,1)S(1)} async-done(((bf16[4,144,512]{2,1,0:T(8,128)(2,1)}), bf16[4,144,512]{2,1,0:T(8,128)(2,1)S(1)}, u32[]{:S(2)}, u32[]{:S(2)}) %all-to-all-start.1) | async-done | bytes 589856 | tf_op jit(solution)/shard_map/all_to_all | solution.py:24
  91.6 0.1 broadcast_in_dim.93
  91.7 4.7 %all_to_all.61 = bf16[2,576,512]{2,1,0:T(8,128)(2,1)S(1)} all-to-all(bf16[2,576,512]{2,1,0:T(8,128)(2,1)S(1)} %broadcast_in_dim.93), channel_id=1, replica_groups=mesh['z'=12,'x'=4,'c'=2,'y'=8] {'c'}, dimensions={0} | all-to-all | bytes 2359296 | tf_op jit(solution)/shard_map/all_to_all | solution.py:24
  96.3 0.9 broadcast_in_dim.97
  97.3 4.9 %all-to-all-start.5 = ((bf16[4,144,512]{2,1,0:T(8,128)(2,1)}), bf16[4,144,512]{2,1,0:T(8,128)(2,1)S(1)}, u32[]{:S(2)}, u32[]{:S(2)}) async-start(bf16[4,144,512]{2,1,0:T(8,128)(2,1)} %broadcast_in_dim.97), calls=%async_computation.6 | async-start | bytes 1179648 | tf_op jit(solution)/shard_map/all_to_all | solution.py:24
  102.2 0.8 convolution_convert_fusion.3
  103.0 0.6 fusion.12
  103.6 7.9 %all-to-all-done.5 = bf16[4,144,512]{2,1,0:T(8,128)(2,1)S(1)} async-done(((bf16[4,144,512]{2,1,0:T(8,128)(2,1)}), bf16[4,144,512]{2,1,0:T(8,128)(2,1)S(1)}, u32[]{:S(2)}, u32[]{:S(2)}) %all-to-all-start.5) | async-done | bytes 589856 | tf_op jit(solution)/shard_map/all_to_all | solution.py:24
  111.6 4.7 %all_to_all.62 = bf16[2,576,512]{2,1,0:T(8,128)(2,1)S(1)} all-to-all(bf16[2,576,512]{2,1,0:T(8,128)(2,1)S(1)} %broadcast_in_dim.99), channel_id=1, replica_groups=mesh['z'=12,'x'=4,'c'=2,'y'=8] {'c'}, dimensions={0} | all-to-all | bytes 2359296 | tf_op jit(solution)/shard_map/all_to_all | solution.py:24
  116.2 0.6 fusion.11
  116.8 0.6 broadcast_in_dim.100
  117.4 3.3 %all-to-all-start.7 = ((f32[8,2,256]{2,1,0:T(2,128)}), f32[8,2,256]{2,1,0:T(2,128)S(1)}, u32[]{:S(2)}, u32[]{:S(2)}) async-start(f32[8,2,256]{2,1,0:T(2,128)} %broadcast_in_dim.100), calls=%async_computation.8 | async-start | bytes 32768 | tf_op jit(solution)/shard_map/all_to_all | solution.py:24
  120.8 0.1 select_reduce_fusion
  120.9 0.1 copy.23
  121.0 7.5 %all-to-all-done.7 = f32[8,2,256]{2,1,0:T(2,128)S(1)} async-done(((f32[8,2,256]{2,1,0:T(2,128)}), f32[8,2,256]{2,1,0:T(2,128)S(1)}, u32[]{:S(2)}, u32[]{:S(2)}) %all-to-all-start.7) | async-done | bytes 16416 | tf_op jit(solution)/shard_map/all_to_all | solution.py:24
  128.6 0.7 convolution_convert_fusion.2
  129.3 4.9 %all_to_all.63 = bf16[2,576,640]{2,1,0:T(8,128)(2,1)S(1)} all-to-all(bf16[2,576,640]{2,1,0:T(8,128)(2,1)S(1)} %bitcast.52), channel_id=1, replica_groups=mesh['z'=12,'x'=4,'c'=2,'y'=8] {'c'}, dimensions={0} | all-to-all | bytes 2949120 | tf_op jit(solution)/shard_map/all_to_all | solution.py:28
  134.2 0.7 reduce_sum.108
  134.9 14.7 %all_to_all.64 = bf16[4,144,640]{2,1,0:T(8,128)(2,1)S(1)} all-to-all(bf16[4,144,640]{2,1,0:T(8,128)(2,1)S(1)} %bitcast.53), channel_id=1, replica_groups=mesh['z'=12,'x'=4,'c'=2,'y'=8] {'x'}, dimensions={0} | all-to-all | bytes 1474560 | tf_op jit(solution)/shard_map/all_to_all | solution.py:28
  149.6 0.1 reduce_sum.109
  149.7 0.7 convert_element_type.93
  150.5 3.5 %all-to-all-start.10 = ((bf16[12,12,640]{2,1,0:T(8,128)(2,1)}), bf16[12,12,640]{2,1,0:T(8,128)(2,1)S(1)}, u32[]{:S(2)}, u32[]{:S(2)}) async-start(bf16[12,12,640]{2,1,0:T(8,128)(2,1)} %convert_element_type.93), calls=%async_computation.11 | async-start | bytes 491520 | tf_op jit(solution)/shard_map/all_to_all | solution.py:28
  154.0 0.1 dynamic_slice.7
  154.1 15.8 %all-to-all-done.10 = bf16[12,12,640]{2,1,0:T(8,128)(2,1)S(1)} async-done(((bf16[12,12,640]{2,1,0:T(8,128)(2,1)}), bf16[12,12,640]{2,1,0:T(8,128)(2,1)S(1)}, u32[]{:S(2)}, u32[]{:S(2)}) %all-to-all-start.10) | async-done | bytes 184352 | tf_op jit(solution)/shard_map/all_to_all | solution.py:28
  170.0 3.5 %convolution_convert_fusion.1 = bf16[12,4096]{1,0:T(8,128)(2,1)S(1)} fusion(bf16[4096,512]{1,0:T(8,128)(2,1)} %param.12, bf16[12,640]{1,0:T(8,128)(2,1)S(1)} %reduce_sum.110), kind=kOutput, calls=%fused_computation.4 | convolution fusion | flops 50380800 | bytes 4308992 | tf_op jit(solution)/shard_map/dot_general | solution.py:18
  173.6 0.7 pad_maximum_fusion
  174.3 3.4 %all-to-all-start.11 = ((bf16[8,12,640]{2,1,0:T(8,128)(2,1)}), bf16[8,12,640]{2,1,0:T(8,128)(2,1)S(1)}, u32[]{:S(2)}, u32[]{:S(2)}) async-start(bf16[8,12,640]{2,1,0:T(8,128)(2,1)} %pad_maximum_fusion), calls=%async_computation.12 | async-start | bytes 327680 | tf_op jit(solution)/shard_map/all_to_all | solution.py:104
  177.7 1.5 fusion.10
  179.2 7.8 %all-to-all-done.11 = bf16[8,12,640]{2,1,0:T(8,128)(2,1)S(1)} async-done(((bf16[8,12,640]{2,1,0:T(8,128)(2,1)}), bf16[8,12,640]{2,1,0:T(8,128)(2,1)S(1)}, u32[]{:S(2)}, u32[]{:S(2)}) %all-to-all-start.11) | async-done | bytes 122912 | tf_op jit(solution)/shard_map/all_to_all | solution.py:104
  187.0 0.2 fusion.13
  187.3 0.6 reshape.220
  187.9 1.7 fusion.5
  189.6 1.3 fusion.8
  (44 shorter events, 0.7 us)
Async XLA Ops:
  7.2 77.8 %copy-start = (bf16[256,1024]{1,0:T(8,128)(2,1)S(1)}, bf16[256,1024]{1,0:T(8,128)(2,1)}, u32[]{:S(2)}) copy-start(bf16[256,1024]{1,0:T(8,128)(2,1)} %param.7) | copy-start | bytes 1572868
  7.2 180.7 %reduce-scatter.2.cloned.1.call-start = ((), (), s32[]{:S(2)}) async-start(), calls=%async_computation.13 | async-start | bytes 7077888 | tf_op jit(solution)/shard_map/reduce_scatter | solution.py:56
  16.3 0.7 copy-start.6
  16.3 32.6 %copy-start.5 = (f32[4096]{0:T(1024)S(1)}, f32[4096]{0:T(1024)}, u32[]{:S(2)}) copy-start(f32[4096]{0:T(1024)} %param.11) | copy-start | bytes 49156
  33.7 27.9 %all-to-all-start = ((bf16[12,12,512]{2,1,0:T(8,128)(2,1)}), bf16[12,12,512]{2,1,0:T(8,128)(2,1)S(1)}, u32[]{:S(2)}, u32[]{:S(2)}) async-start(bf16[12,12,512]{2,1,0:T(8,128)(2,1)} %broadcast_in_dim.48), calls=%async_computation.1 | async-start | bytes 393216 | tf_op jit(solution)/shard_map/all_to_all | solution.py:24
  62.3 16.6 %all-to-all-start.4 = ((bf16[12,12,512]{2,1,0:T(8,128)(2,1)}), bf16[12,12,512]{2,1,0:T(8,128)(2,1)S(1)}, u32[]{:S(2)}, u32[]{:S(2)}) async-start(bf16[12,12,512]{2,1,0:T(8,128)(2,1)} %broadcast_in_dim.95), calls=%async_computation.5 | async-start | bytes 393216 | tf_op jit(solution)/shard_map/all_to_all | solution.py:24
  79.8 11.8 %all-to-all-start.1 = ((bf16[4,144,512]{2,1,0:T(8,128)(2,1)}), bf16[4,144,512]{2,1,0:T(8,128)(2,1)S(1)}, u32[]{:S(2)}, u32[]{:S(2)}) async-start(bf16[4,144,512]{2,1,0:T(8,128)(2,1)} %broadcast_in_dim.50), calls=%async_computation.2 | async-start | bytes 1179648 | tf_op jit(solution)/shard_map/all_to_all | solution.py:24
  96.3 6.7 %copy-start.3 = (bf16[2,576,512]{2,1,0:T(8,128)(2,1)}, bf16[2,576,512]{2,1,0:T(8,128)(2,1)S(1)}, u32[]{:S(2)}) copy-start(bf16[2,576,512]{2,1,0:T(8,128)(2,1)S(1)} %all_to_all.61) | copy-start | bytes 3538948
  97.3 14.2 %all-to-all-start.5 = ((bf16[4,144,512]{2,1,0:T(8,128)(2,1)}), bf16[4,144,512]{2,1,0:T(8,128)(2,1)S(1)}, u32[]{:S(2)}, u32[]{:S(2)}) async-start(bf16[4,144,512]{2,1,0:T(8,128)(2,1)} %broadcast_in_dim.97), calls=%async_computation.6 | async-start | bytes 1179648 | tf_op jit(solution)/shard_map/all_to_all | solution.py:24
  116.2 4.5 %copy-start.7 = (s32[8]{0:T(128)S(1)}, s32[8]{0:T(128)}, u32[]{:S(2)}) copy-start(s32[8]{0:T(128)} %param.8) | copy-start | bytes 100
  117.4 11.0 %all-to-all-start.7 = ((f32[8,2,256]{2,1,0:T(2,128)}), f32[8,2,256]{2,1,0:T(2,128)S(1)}, u32[]{:S(2)}, u32[]{:S(2)}) async-start(f32[8,2,256]{2,1,0:T(2,128)} %broadcast_in_dim.100), calls=%async_computation.8 | async-start | bytes 32768 | tf_op jit(solution)/shard_map/all_to_all | solution.py:24
  150.5 19.4 %all-to-all-start.10 = ((bf16[12,12,640]{2,1,0:T(8,128)(2,1)}), bf16[12,12,640]{2,1,0:T(8,128)(2,1)S(1)}, u32[]{:S(2)}, u32[]{:S(2)}) async-start(bf16[12,12,640]{2,1,0:T(8,128)(2,1)} %convert_element_type.93), calls=%async_computation.11 | async-start | bytes 491520 | tf_op jit(solution)/shard_map/all_to_all | solution.py:28
  170.0 7.7 %copy-start.4 = (bf16[2,576,512]{2,1,0:T(8,128)(2,1)S(1)}, bf16[2,576,512]{2,1,0:T(8,128)(2,1)}, u32[]{:S(2)}) copy-start(bf16[2,576,512]{2,1,0:T(8,128)(2,1)} %copy-done.3) | copy-start | bytes 3538948
  174.3 12.7 %all-to-all-start.11 = ((bf16[8,12,640]{2,1,0:T(8,128)(2,1)}), bf16[8,12,640]{2,1,0:T(8,128)(2,1)S(1)}, u32[]{:S(2)}, u32[]{:S(2)}) async-start(bf16[8,12,640]{2,1,0:T(8,128)(2,1)} %pad_maximum_fusion), calls=%async_computation.12 | async-start | bytes 327680 | tf_op jit(solution)/shard_map/all_to_all | solution.py:104
  179.2 8.7 %copy-start.1 = (bf16[96,4096]{1,0:T(8,128)(2,1)S(1)}, bf16[96,4096]{1,0:T(8,128)(2,1)}, u32[]{:S(2)}) copy-start(bf16[96,4096]{1,0:T(8,128)(2,1)} %param.10) | copy-start | bytes 2359300
  187.9 1.7 copy-start.2
Sparse Core Ops, SparseCore 0:
  16.4 86.8 reduce-scatter.1

commit v3 on v2

v3 whole, which is shorter than its diff:
```python
import jax
import jax.numpy as jnp
from jax import lax
from jax.sharding import Mesh
from jax.sharding import PartitionSpec as P


IMG_MAX = 4
PATCH = 8
DP = ("z", "x", "c")
DP_MP = ("z", "x", "c", "y")

norm_eps = 1e-05
bf16 = jnp.bfloat16
f32 = jnp.float32


def dot(left, right, left_dim, right_dim):
    return lax.dot_general(
        left, right, (((left_dim,), (right_dim,)), ((), ())), preferred_element_type=f32
    )


def spread(block, axis):
    n = lax.axis_size(axis)
    copies = jnp.broadcast_to(block[None], (n, *block.shape))
    return lax.all_to_all(copies, axis, split_axis=0, concat_axis=0, tiled=True)


def summed(blocks, axis):
    parts = lax.all_to_all(blocks.astype(bf16), axis, split_axis=0, concat_axis=0, tiled=True)
    return jnp.sum(parts.astype(f32), axis=0)


def swapped(block):
    return lax.ppermute(block, "c", [(0, 1), (1, 0)])


def shift(value, axis, by):
    n = lax.axis_size(axis)
    return lax.ppermute(value, axis, [(i, (i + by) % n) for i in range(n)])


def column_sum(part, axis):
    n = lax.axis_size(axis)
    me = lax.axis_index(axis)
    size = part.shape[0] // n
    half = size // 2

    def chunk(k, start=0, count=size):
        return lax.dynamic_slice_in_dim(part, (me + k) % n * size + start, count, 0)

    near_up = shift(jnp.concatenate([chunk(3), chunk(1)], axis=0), axis, 1)
    near_down = shift(jnp.concatenate([chunk(-3), chunk(-1)], axis=0), axis, -1)
    far_up = shift(chunk(4, 0, half), axis, 2)
    far_down = shift(chunk(4, half, half), axis, -2)
    rest = jnp.zeros((half, part.shape[1]), f32)
    up = jnp.concatenate([far_up.astype(f32), rest], axis=0)
    up = (up + chunk(2).astype(f32) + near_up[:size].astype(f32)).astype(part.dtype)
    up = shift(up, axis, 2)
    down = jnp.concatenate([rest, far_down.astype(f32)], axis=0)
    down = (down + chunk(-2).astype(f32) + near_down[:size].astype(f32)).astype(part.dtype)
    down = shift(down, axis, -2)
    near = chunk(0).astype(f32) + near_up[size:].astype(f32) + near_down[size:].astype(f32)
    return near + up.astype(f32) + down.astype(f32)


def compute(vision_rows, image_count, proj_flat, text_embeds, norm_gain, q_weight, q_grad):
    groups = lax.axis_size("y")
    member = lax.axis_index("y")
    nz, nx, nc = (lax.axis_size(a) for a in DP)
    shards = nz * nx * nc
    enc = vision_rows.shape[1]
    cols = q_weight.shape[1]
    width = q_weight.shape[0]
    image_rows = IMG_MAX * PATCH
    own_rows = q_grad.shape[0] // groups
    text_rows = own_rows - image_rows
    per_shard = proj_flat.shape[0] * 128 // cols
    half = nx * nz * per_shard

    rows = spread(proj_flat.reshape(per_shard, cols), "z")
    rows = rows.reshape(nz * per_shard, cols)
    rows = spread(rows, "x")
    rows = rows.reshape(half, cols)
    proj = jnp.concatenate([rows, swapped(rows)], axis=0)

    q_own = q_grad.reshape(groups, own_rows, cols)
    q_image = q_own[:, :image_rows].reshape(groups * image_rows, cols)
    q_text = q_own[:, image_rows:].reshape(groups * text_rows, cols)
    image_part = dot(q_weight, q_image, 1, 1).astype(bf16)
    image_norm = column_sum(image_part, "y")
    text_part = dot(q_text, q_weight, 1, 1).astype(bf16)
    text_norm = lax.psum_scatter(text_part, "y", scatter_dimension=0, tiled=True)

    order = jnp.arange(shards * per_shard, dtype=jnp.int32)
    row = order % per_shard
    zi = order // per_shard % nz
    xi = order // (per_shard * nz) % nx
    ci = (order // half + lax.axis_index("c")) % nc
    source = ((zi * nx + xi) * nc + ci) * per_shard + row
    pick = (jnp.arange(enc, dtype=jnp.int32)[:, None] == source[None, :]).astype(bf16)
    vision = dot(vision_rows, pick, 1, 0).astype(bf16)
    embed = dot(proj, vision, 0, 1).astype(bf16)
    squares = jnp.sum(jnp.square(embed.astype(f32)), axis=0)
    embed, squares = lax.optimization_barrier((embed, squares))
    inputs = embed.astype(f32)

    gain_own = lax.dynamic_slice_in_dim(norm_gain, member * cols, cols, 0)
    scaled = gain_own[:, None] * image_norm
    stats = jnp.stack([squares, jnp.sum(scaled * inputs, axis=0)])
    stats = spread(stats, "y")
    stats = jnp.sum(stats, axis=0) / width
    inv_rms = lax.rsqrt(stats[0] + norm_eps)
    row_ids = jnp.arange(groups * image_rows, dtype=jnp.int32)
    owner_match = (row_ids // image_rows)[:, None] == jnp.arange(groups, dtype=jnp.int32)[None, :]
    counts = jnp.sum(jnp.where(owner_match, image_count[None, :], 0), axis=1)
    live = row_ids % image_rows // PATCH < counts
    image_grad = inv_rms[None, :] * scaled - inputs * (inv_rms**3 * stats[1])[None, :]
    grad_scale = 1.0 / jnp.sqrt(f32(shards * groups * image_rows))
    image_grad = jnp.where(live[None, :], image_grad * grad_scale, 0.0).astype(bf16)
    other = dot(vision[:, half:], image_grad, 0, 1).astype(bf16)
    other = swapped(other)
    part = dot(vision[:, :half], image_grad, 0, 1) + other.astype(f32)
    part = summed(part.reshape(nx, nz * per_shard, cols), "x")
    part = summed(part.reshape(nz, per_shard, cols), "z")
    proj_grad = part.reshape(proj_flat.shape)

    text_in = text_embeds.astype(f32)
    text_rms = lax.rsqrt(jnp.mean(text_in * text_in, axis=-1, keepdims=True) + norm_eps)
    text_scaled = norm_gain[None, :] * text_norm.astype(f32)
    inner = jnp.mean(text_scaled * text_in, axis=-1, keepdims=True)
    text_grad = (text_rms * text_scaled - text_in * text_rms**3 * inner).astype(bf16)
    return (text_grad, proj_grad)


def solution(mesh):
    finer = Mesh(mesh.devices.reshape(12, 4, 2, mesh.shape["mp"]), DP_MP)
    placed = (P(DP, None), P(DP), P(DP_MP, None), P(DP_MP, None), P(), P(None, "y"), P(DP, "y"))
    return jax.shard_map(
        compute,
        mesh=finer,
        in_specs=placed,
        out_specs=(P(DP_MP, None), P(DP_MP, None)),
        check_vma=False,
    )
```

time: 199 us -> 189 us (0.950)
  the two profiles are of different devices: /device:TPU:2 before, /device:TPU:64 now
where the time goes in v3:
time: 189 us; the launch traced here: 188 us
  waiting for transfers between devices  55.7 us (29%)
  starting transfers between devices  52.7 us (28%)
  blocking collectives  30.7 us (16%)
  matrix products  15.4 us (8%)
  between operations  14.4 us (8%)
  other arithmetic  10.6 us (6%)
  local copies, waits for them, and re-layouts  8.24 us (4%)
    ppermute x6, waiting for transfers between devices, shift(): return lax.ppermute(value, axis, [(i, (i + by) % n) for i in range(n)])  37.6 us
    all_to_all x2, blocking collectives, summed(): lax.all_to_all(blocks.astype(bf16), axis, split_axis=0, concat_axis=0, ti...  30.7 us
    all_to_all x3, starting transfers between devices, spread(): return lax.all_to_all(copies, axis, split_axis=0, concat_axis=0, tiled=True)  24.7 us
    ppermute x6, starting transfers between devices, shift(): return lax.ppermute(value, axis, [(i, (i + by) % n) for i in range(n)])  24.2 us
    all_to_all x3, waiting for transfers between devices, spread(): return lax.all_to_all(copies, axis, split_axis=0, concat_axis=0, tiled=True)  16.1 us
    dot_general x6, matrix products, dot(): lax.dot_general(left, right, (((left_dim,), (right_dim,)), ((), ())), pre...  15.4 us
    ppermute x2, starting transfers between devices, swapped(): return lax.ppermute(block, 'c', [(0, 1), (1, 0)])  3.84 us
  transfers between devices with their start and end apart: 12, of which 7 were waited for; matrix products, arithmetic and copies ran while one was open for 12% of the time, Pallas kernels for 0%

profile of v3, /device:TPU:64, one launch (start us, length us, event | category | flops | bytes accessed | tf_op | source)
XLA Modules:
  0.0 187.7 jit_solution(3509060592658113493)
XLA Ops:
  7.2 0.0 reduce-scatter.2.cloned.1.call-start
  7.2 1.2 slice.40
  8.5 7.5 %convolution_convert_fusion = bf16[768,4096]{1,0:T(8,128)(2,1)} fusion(bf16[768,512]{1,0:T(8,128)(2,1)S(1)} %bitcast.21, bf16[4096,512]{1,0:T(8,128)(2,1)} %param.12), kind=kOutput, calls=%fused_computation | convolution fusion | flops 3224371200 | bytes 11272192 | tf_op jit(solution)/shard_map/dot_general | solution.py:19
  16.0 0.0 reduce-scatter.2.cloned.1.call-update
  16.0 0.7 copy-done.6
  16.7 0.7 broadcast_in_dim.38
  17.4 14.8 %all-to-all-start = ((bf16[12,12,512]{2,1,0:T(8,128)(2,1)}), bf16[12,12,512]{2,1,0:T(8,128)(2,1)}, u32[]{:S(2)}, u32[]{:S(2)}) async-start(bf16[12,12,512]{2,1,0:T(8,128)(2,1)} %broadcast_in_dim.38), calls=%async_computation.1 | async-start | bytes 393216 | tf_op jit(solution)/shard_map/all_to_all | solution.py:27
  32.2 1.0 slice.42
  33.3 3.5 %convolution_convert_fusion.1 = bf16[4096,256]{1,0:T(8,128)(2,1)S(1)} fusion(bf16[4096,512]{1,0:T(8,128)(2,1)} %param.12, bf16[256,512]{1,0:T(8,128)(2,1)S(1)} %bitcast.24), kind=kOutput, calls=%fused_computation.1 | convolution fusion | flops 1074790400 | bytes 6553600 | tf_op jit(solution)/shard_map/dot_general | solution.py:19
  36.7 0.8 constant_dynamic-slice_fusion.5
  37.5 8.3 %all-to-all-done = bf16[12,12,512]{2,1,0:T(8,128)(2,1)} async-done(((bf16[12,12,512]{2,1,0:T(8,128)(2,1)}), bf16[12,12,512]{2,1,0:T(8,128)(2,1)}, u32[]{:S(2)}, u32[]{:S(2)}) %all-to-all-start) | async-done | bytes 147488 | tf_op jit(solution)/shard_map/all_to_all | solution.py:27
  45.8 1.0 broadcast_in_dim.62
  46.8 0.9 broadcast_in_dim.63
  47.7 4.3 %all-to-all-start.1 = ((bf16[4,144,512]{2,1,0:T(8,128)(2,1)}), bf16[4,144,512]{2,1,0:T(8,128)(2,1)}, u32[]{:S(2)}, u32[]{:S(2)}) async-start(bf16[4,144,512]{2,1,0:T(8,128)(2,1)} %broadcast_in_dim.63), calls=%async_computation.2 | async-start | bytes 1179648 | tf_op jit(solution)/shard_map/all_to_all | solution.py:27
  52.0 0.9 pad_maximum_fusion
  52.9 3.5 %collective-permute-start.1 = (bf16[1024,256]{1,0:T(8,128)(2,1)}, bf16[1024,256]{1,0:T(8,128)(2,1)S(1)}, u32[]{:S(2)}, u32[]{:S(2)}) collective-permute-start(bf16[1024,256]{1,0:T(8,128)(2,1)} %pad_maximum_fusion), channel_id=1, source_target_pairs={{0,1},{1,2},{2,3},{3,4},{4,5},{5,6},{6,7},{7,0},{8,9},{9,10},{10,1... | collective-permute-start | bytes 1572872 | tf_op jit(solution)/shard_map/ppermute | solution.py:41
  56.4 1.8 pad_maximum_fusion.1
  58.1 3.8 %collective-permute-start.2 = (bf16[1024,256]{1,0:T(8,128)(2,1)}, bf16[1024,256]{1,0:T(8,128)(2,1)}, u32[]{:S(2)}, u32[]{:S(2)}) collective-permute-start(bf16[1024,256]{1,0:T(8,128)(2,1)} %pad_maximum_fusion.1), channel_id=1, source_target_pairs={{0,7},{1,0},{2,1},{3,2},{4,3},{5,4},{6,5},{7,6},{8,15},{9,8},{10,9... | collective-permute-start | bytes 1572872 | tf_op jit(solution)/shard_map/ppermute | solution.py:41
  62.0 0.7 constant_dynamic-slice_fusion.1
  62.6 3.0 %collective-permute-start.3 = (bf16[256,256]{1,0:T(8,128)(2,1)}, bf16[256,256]{1,0:T(8,128)(2,1)S(1)}, u32[]{:S(2)}, u32[]{:S(2)}) collective-permute-start(bf16[256,256]{1,0:T(8,128)(2,1)} %get-tuple-element.10), channel_id=1, source_target_pairs={{0,2},{1,3},{2,4},{3,5},{4,6},{5,7},{6,0},{7,1},{8,10},{9,11},{10,... | collective-permute-start | bytes 393224 | tf_op jit(solution)/shard_map/ppermute | solution.py:41
  65.7 4.9 %collective-permute-start.5 = (bf16[256,256]{1,0:T(8,128)(2,1)S(1)}, bf16[256,256]{1,0:T(8,128)(2,1)S(1)}, u32[]{:S(2)}, u32[]{:S(2)}) collective-permute-start(bf16[256,256]{1,0:T(8,128)(2,1)S(1)} %get-tuple-element.11), channel_id=1, source_target_pairs={{0,6},{1,7},{2,0},{3,1},{4,2},{5,3},{6,4},{7,5},{8,14},{9,15},{10,... | collective-permute-start | bytes 393224 | tf_op jit(solution)/shard_map/ppermute | solution.py:41
  70.6 1.9 %collective-permute-start = (bf16[576,512]{1,0:T(8,128)(2,1)}, bf16[576,512]{1,0:T(8,128)(2,1)}, u32[]{:S(2)}, u32[]{:S(2)}) collective-permute-start(bf16[576,512]{1,0:T(8,128)(2,1)} %bitcast.3), channel_id=1, source_target_pairs={{0,8},{8,0},{1,9},{9,1},{2,10},{10,2},{3,11},{11,3},{4,12},{12,4},... | collective-permute-start | bytes 1769480 | tf_op jit(solution)/shard_map/ppermute | solution.py:36
  72.6 1.7 convolution_convert_fusion.2
  74.2 17.3 %collective-permute-done.3 = bf16[256,256]{1,0:T(8,128)(2,1)S(1)} collective-permute-done((bf16[256,256]{1,0:T(8,128)(2,1)}, bf16[256,256]{1,0:T(8,128)(2,1)S(1)}, u32[]{:S(2)}, u32[]{:S(2)}) %collective-permute-start.3) | collective-permute-done | bytes 131104 | tf_op jit(solution)/shard_map/ppermute | solution.py:41
  91.5 3.4 %collective-permute-done.5 = bf16[256,256]{1,0:T(8,128)(2,1)S(1)} collective-permute-done((bf16[256,256]{1,0:T(8,128)(2,1)S(1)}, bf16[256,256]{1,0:T(8,128)(2,1)S(1)}, u32[]{:S(2)}, u32[]{:S(2)}) %collective-permute-start.5) | collective-permute-done | bytes 131104 | tf_op jit(solution)/shard_map/ppermute | solution.py:41
  95.0 1.9 %add_convert_fusion.2 = (bf16[512,256]{1,0:T(8,128)(2,1)}, bf16[512,256]{1,0:T(8,128)(2,1)}) fusion(bf16[1024,256]{1,0:T(8,128)(2,1)S(1)} %collective-permute-done.1, bf16[4096,256]{1,0:T(8,128)(2,1)S(1)} %convolution_convert_fusion.1, s32[]{:T(128)S(6)} %select_n.183, bf16[256,256]{1,0:T(8,128)(2,1)S(1)} %collective-permute-done.3, ...), kind=kLoop, calls=%fused_computation.32 | loop fusion | flops 1572864 | bytes 1835016 | tf_op jit(solution)/shard_map/convert_element_type | solution.py:59
  96.9 5.2 %collective-permute-start.6 = (bf16[512,256]{1,0:T(8,128)(2,1)}, bf16[512,256]{1,0:T(8,128)(2,1)S(1)}, u32[]{:S(2)}, u32[]{:S(2)}) collective-permute-start(bf16[512,256]{1,0:T(8,128)(2,1)} %get-tuple-element.9), channel_id=1, source_target_pairs={{0,6},{1,7},{2,0},{3,1},{4,2},{5,3},{6,4},{7,5},{8,14},{9,15},{10,... | collective-permute-start | bytes 786440 | tf_op jit(solution)/shard_map/ppermute | solution.py:41
  102.1 3.8 %collective-permute-start.4 = (bf16[512,256]{1,0:T(8,128)(2,1)}, bf16[512,256]{1,0:T(8,128)(2,1)}, u32[]{:S(2)}, u32[]{:S(2)}) collective-permute-start(bf16[512,256]{1,0:T(8,128)(2,1)} %get-tuple-element.8), channel_id=1, source_target_pairs={{0,2},{1,3},{2,4},{3,5},{4,6},{5,7},{6,0},{7,1},{8,10},{9,11},{10,... | collective-permute-start | bytes 786440 | tf_op jit(solution)/shard_map/ppermute | solution.py:41
  105.9 0.1 select_reduce_fusion
  106.0 0.1 dynamic_slice.30
  106.1 2.0 %multiply_reduce_fusion = (f32[256]{0:T(256)S(1)}, bf16[512,256]{1,0:T(8,128)(2,1)S(1)}) fusion(bf16[1152,256]{1,0:T(8,128)(2,1)} %convolution_convert_fusion.2, bf16[576,512]{1,0:T(8,128)(2,1)} %collective-permute-done, bf16[576,512]{1,0:T(8,128)(2,1)} %bitcast.3), kind=kOutput, calls=%fused_computation.33 | convolution fusion | flops 304873216 | bytes 2032640 | tf_op jit(solution)/shard_map/dot_general | solution.py:19
  108.1 12.5 %collective-permute-done.6 = bf16[512,256]{1,0:T(8,128)(2,1)S(1)} collective-permute-done((bf16[512,256]{1,0:T(8,128)(2,1)}, bf16[512,256]{1,0:T(8,128)(2,1)S(1)}, u32[]{:S(2)}, u32[]{:S(2)}) %collective-permute-start.6) | collective-permute-done | bytes 262176 | tf_op jit(solution)/shard_map/ppermute | solution.py:41
  120.6 4.4 %collective-permute-done.4 = bf16[512,256]{1,0:T(8,128)(2,1)} collective-permute-done((bf16[512,256]{1,0:T(8,128)(2,1)}, bf16[512,256]{1,0:T(8,128)(2,1)}, u32[]{:S(2)}, u32[]{:S(2)}) %collective-permute-start.4) | collective-permute-done | bytes 262176 | tf_op jit(solution)/shard_map/ppermute | solution.py:41
  125.0 1.3 fusion.11
  126.2 0.6 broadcast_in_dim.64
  126.9 5.6 %all-to-all-start.2 = ((f32[8,2,256]{2,1,0:T(2,128)}), f32[8,2,256]{2,1,0:T(2,128)S(1)}, u32[]{:S(2)}, u32[]{:S(2)}) async-start(f32[8,2,256]{2,1,0:T(2,128)} %broadcast_in_dim.64), calls=%async_computation.3 | async-start | bytes 32768 | tf_op jit(solution)/shard_map/all_to_all | solution.py:27
  132.5 7.8 %all-to-all-done.2 = f32[8,2,256]{2,1,0:T(2,128)S(1)} async-done(((f32[8,2,256]{2,1,0:T(2,128)}), f32[8,2,256]{2,1,0:T(2,128)S(1)}, u32[]{:S(2)}, u32[]{:S(2)}) %all-to-all-start.2) | async-done | bytes 16416 | tf_op jit(solution)/shard_map/all_to_all | solution.py:27
  140.3 1.5 fusion.15
  141.7 0.3 convolution_convert_fusion.3
  142.1 1.9 %collective-permute-start.7 = (bf16[576,512]{1,0:T(8,128)(2,1)S(1)}, bf16[576,512]{1,0:T(8,128)(2,1)S(1)}, u32[]{:S(2)}, u32[]{:S(2)}) collective-permute-start(bf16[576,512]{1,0:T(8,128)(2,1)S(1)} %convolution_convert_fusion.3), channel_id=1, source_target_pairs={{0,8},{8,0},{1,9},{9,1},{2,10},{10,2},{3,11},{11,3},{4,12},{12,4},... | collective-permute-start | bytes 1769480 | tf_op jit(solution)/shard_map/ppermute | solution.py:36
  144.0 2.0 %collective-permute-done.7 = bf16[576,512]{1,0:T(8,128)(2,1)S(1)} collective-permute-done((bf16[576,512]{1,0:T(8,128)(2,1)S(1)}, bf16[576,512]{1,0:T(8,128)(2,1)S(1)}, u32[]{:S(2)}, u32[]{:S(2)}) %collective-permute-start.7) | collective-permute-done | bytes 589856 | tf_op jit(solution)/shard_map/ppermute | solution.py:36
  146.0 0.3 add_convert_fusion
  146.4 14.9 %all_to_all.25 = bf16[4,144,512]{2,1,0:T(8,128)(2,1)S(1)} all-to-all(bf16[4,144,512]{2,1,0:T(8,128)(2,1)S(1)} %bitcast.18), channel_id=1, replica_groups=mesh['z'=12,'x'=4,'c'=2,'y'=8] {'x'}, dimensions={0} | all-to-all | bytes 1179648 | tf_op jit(solution)/shard_map/all_to_all | solution.py:31
  161.3 0.1 reduce_sum.81
  161.4 15.8 %all_to_all.26 = bf16[12,12,512]{2,1,0:T(8,128)(2,1)S(1)} all-to-all(bf16[12,12,512]{2,1,0:T(8,128)(2,1)S(1)} %convert_element_type.115), channel_id=1, replica_groups=mesh['z'=12,'x'=4,'c'=2,'y'=8] {'z'}, dimensions={0} | all-to-all | bytes 294912 | tf_op jit(solution)/shard_map/all_to_all | solution.py:31
  177.2 0.6 reshape.159
  177.8 1.7 fusion.3
  179.5 1.3 fusion.6
  (32 shorter events, 0.2 us)
Async XLA Ops:
  7.2 65.4 %copy-start = (bf16[256,1024]{1,0:T(8,128)(2,1)S(1)}, bf16[256,1024]{1,0:T(8,128)(2,1)}, u32[]{:S(2)}) copy-start(bf16[256,1024]{1,0:T(8,128)(2,1)} %param.7) | copy-start | bytes 1572868
  7.2 170.7 %reduce-scatter.2.cloned.1.call-start = ((), (), s32[]{:S(2)}) async-start(), calls=%async_computation.6 | async-start | bytes 7077888 | tf_op jit(solution)/shard_map/reduce_scatter | solution.py:94
  16.0 0.7 copy-start.6
  17.4 28.4 %all-to-all-start = ((bf16[12,12,512]{2,1,0:T(8,128)(2,1)}), bf16[12,12,512]{2,1,0:T(8,128)(2,1)}, u32[]{:S(2)}, u32[]{:S(2)}) async-start(bf16[12,12,512]{2,1,0:T(8,128)(2,1)} %broadcast_in_dim.38), calls=%async_computation.1 | async-start | bytes 393216 | tf_op jit(solution)/shard_map/all_to_all | solution.py:27
  47.7 22.9 %all-to-all-start.1 = ((bf16[4,144,512]{2,1,0:T(8,128)(2,1)}), bf16[4,144,512]{2,1,0:T(8,128)(2,1)}, u32[]{:S(2)}, u32[]{:S(2)}) async-start(bf16[4,144,512]{2,1,0:T(8,128)(2,1)} %broadcast_in_dim.63), calls=%async_computation.2 | async-start | bytes 1179648 | tf_op jit(solution)/shard_map/all_to_all | solution.py:27
  52.9 42.1 %collective-permute-start.1 = (bf16[1024,256]{1,0:T(8,128)(2,1)}, bf16[1024,256]{1,0:T(8,128)(2,1)S(1)}, u32[]{:S(2)}, u32[]{:S(2)}) collective-permute-start(bf16[1024,256]{1,0:T(8,128)(2,1)} %pad_maximum_fusion), channel_id=1, source_target_pairs={{0,1},{1,2},{2,3},{3,4},{4,5},{5,6},{6,7},{7,0},{8,9},{9,10},{10,1... | collective-permute-start | bytes 1572872 | tf_op jit(solution)/shard_map/ppermute | solution.py:41
  58.1 36.8 %collective-permute-start.2 = (bf16[1024,256]{1,0:T(8,128)(2,1)}, bf16[1024,256]{1,0:T(8,128)(2,1)}, u32[]{:S(2)}, u32[]{:S(2)}) collective-permute-start(bf16[1024,256]{1,0:T(8,128)(2,1)} %pad_maximum_fusion.1), channel_id=1, source_target_pairs={{0,7},{1,0},{2,1},{3,2},{4,3},{5,4},{6,5},{7,6},{8,15},{9,8},{10,9... | collective-permute-start | bytes 1572872 | tf_op jit(solution)/shard_map/ppermute | solution.py:41
  62.6 28.9 %collective-permute-start.3 = (bf16[256,256]{1,0:T(8,128)(2,1)}, bf16[256,256]{1,0:T(8,128)(2,1)S(1)}, u32[]{:S(2)}, u32[]{:S(2)}) collective-permute-start(bf16[256,256]{1,0:T(8,128)(2,1)} %get-tuple-element.10), channel_id=1, source_target_pairs={{0,2},{1,3},{2,4},{3,5},{4,6},{5,7},{6,0},{7,1},{8,10},{9,11},{10,... | collective-permute-start | bytes 393224 | tf_op jit(solution)/shard_map/ppermute | solution.py:41
  65.7 29.3 %collective-permute-start.5 = (bf16[256,256]{1,0:T(8,128)(2,1)S(1)}, bf16[256,256]{1,0:T(8,128)(2,1)S(1)}, u32[]{:S(2)}, u32[]{:S(2)}) collective-permute-start(bf16[256,256]{1,0:T(8,128)(2,1)S(1)} %get-tuple-element.11), channel_id=1, source_target_pairs={{0,6},{1,7},{2,0},{3,1},{4,2},{5,3},{6,4},{7,5},{8,14},{9,15},{10,... | collective-permute-start | bytes 393224 | tf_op jit(solution)/shard_map/ppermute | solution.py:41
  70.6 35.4 %collective-permute-start = (bf16[576,512]{1,0:T(8,128)(2,1)}, bf16[576,512]{1,0:T(8,128)(2,1)}, u32[]{:S(2)}, u32[]{:S(2)}) collective-permute-start(bf16[576,512]{1,0:T(8,128)(2,1)} %bitcast.3), channel_id=1, source_target_pairs={{0,8},{8,0},{1,9},{9,1},{2,10},{10,2},{3,11},{11,3},{4,12},{12,4},... | collective-permute-start | bytes 1769480 | tf_op jit(solution)/shard_map/ppermute | solution.py:36
  74.2 31.8 %copy-start.5 = (f32[4096]{0:T(1024)S(1)}, f32[4096]{0:T(1024)}, u32[]{:S(2)}) copy-start(f32[4096]{0:T(1024)} %param.11) | copy-start | bytes 49156
  74.2 31.7 %copy-start.7 = (s32[8]{0:T(128)S(1)}, s32[8]{0:T(128)}, u32[]{:S(2)}) copy-start(s32[8]{0:T(128)} %param.8) | copy-start | bytes 100
  96.9 23.7 %collective-permute-start.6 = (bf16[512,256]{1,0:T(8,128)(2,1)}, bf16[512,256]{1,0:T(8,128)(2,1)S(1)}, u32[]{:S(2)}, u32[]{:S(2)}) collective-permute-start(bf16[512,256]{1,0:T(8,128)(2,1)} %get-tuple-element.9), channel_id=1, source_target_pairs={{0,6},{1,7},{2,0},{3,1},{4,2},{5,3},{6,4},{7,5},{8,14},{9,15},{10,... | collective-permute-start | bytes 786440 | tf_op jit(solution)/shard_map/ppermute | solution.py:41
  102.1 22.9 %collective-permute-start.4 = (bf16[512,256]{1,0:T(8,128)(2,1)}, bf16[512,256]{1,0:T(8,128)(2,1)}, u32[]{:S(2)}, u32[]{:S(2)}) collective-permute-start(bf16[512,256]{1,0:T(8,128)(2,1)} %get-tuple-element.8), channel_id=1, source_target_pairs={{0,2},{1,3},{2,4},{3,5},{4,6},{5,7},{6,0},{7,1},{8,10},{9,11},{10,... | collective-permute-start | bytes 786440 | tf_op jit(solution)/shard_map/ppermute | solution.py:41
  108.1 16.9 %copy-start.3 = (bf16[512,256]{1,0:T(8,128)(2,1)}, bf16[512,256]{1,0:T(8,128)(2,1)S(1)}, u32[]{:S(2)}) copy-start(bf16[512,256]{1,0:T(8,128)(2,1)S(1)} %get-tuple-element.5) | copy-start | bytes 786436
  126.9 13.4 %all-to-all-start.2 = ((f32[8,2,256]{2,1,0:T(2,128)}), f32[8,2,256]{2,1,0:T(2,128)S(1)}, u32[]{:S(2)}, u32[]{:S(2)}) async-start(f32[8,2,256]{2,1,0:T(2,128)} %broadcast_in_dim.64), calls=%async_computation.3 | async-start | bytes 32768 | tf_op jit(solution)/shard_map/all_to_all | solution.py:27
  140.2 1.5 copy-start.4
  142.1 3.9 %collective-permute-start.7 = (bf16[576,512]{1,0:T(8,128)(2,1)S(1)}, bf16[576,512]{1,0:T(8,128)(2,1)S(1)}, u32[]{:S(2)}, u32[]{:S(2)}) collective-permute-start(bf16[576,512]{1,0:T(8,128)(2,1)S(1)} %convolution_convert_fusion.3), channel_id=1, source_target_pairs={{0,8},{8,0},{1,9},{9,1},{2,10},{10,2},{3,11},{11,3},{4,12},{12,4},... | collective-permute-start | bytes 1769480 | tf_op jit(solution)/shard_map/ppermute | solution.py:36
  146.4 31.5 %copy-start.1 = (bf16[96,4096]{1,0:T(8,128)(2,1)S(1)}, bf16[96,4096]{1,0:T(8,128)(2,1)}, u32[]{:S(2)}) copy-start(bf16[96,4096]{1,0:T(8,128)(2,1)} %param.10) | copy-start | bytes 2359300
  177.8 1.7 copy-start.2
Sparse Core Ops, SparseCore 0:
  16.2 114.2 reduce-scatter.1

commit v4 on v3

--- a/solution.py
+++ b/solution.py
@@ -79,7 +79,7 @@
     per_shard = proj_flat.shape[0] * 128 // cols
     half = nx * nz * per_shard
 
-    rows = spread(proj_flat.reshape(per_shard, cols), "z")
+    rows = spread(proj_flat, "z")
     rows = rows.reshape(nz * per_shard, cols)
     rows = spread(rows, "x")
     rows = rows.reshape(half, cols)
@@ -89,6 +89,7 @@
     q_image = q_own[:, :image_rows].reshape(groups * image_rows, cols)
     q_text = q_own[:, image_rows:].reshape(groups * text_rows, cols)
     image_part = dot(q_weight, q_image, 1, 1).astype(bf16)
+    image_part, q_text = lax.optimization_barrier((image_part, q_text))
     image_norm = column_sum(image_part, "y")
     text_part = dot(q_text, q_weight, 1, 1).astype(bf16)
     text_norm = lax.psum_scatter(text_part, "y", scatter_dimension=0, tiled=True)
@@ -103,19 +104,20 @@
     vision = dot(vision_rows, pick, 1, 0).astype(bf16)
     embed = dot(proj, vision, 0, 1).astype(bf16)
     squares = jnp.sum(jnp.square(embed.astype(f32)), axis=0)
-    embed, squares = lax.optimization_barrier((embed, squares))
     inputs = embed.astype(f32)
+
+    row_ids = jnp.arange(groups * image_rows, dtype=jnp.int32)
+    owner_match = (row_ids // image_rows)[:, None] == jnp.arange(groups, dtype=jnp.int32)[None, :]
+    counts = jnp.sum(jnp.where(owner_match, image_count[None, :], 0), axis=1)
+    live = row_ids % image_rows // PATCH < counts
 
     gain_own = lax.dynamic_slice_in_dim(norm_gain, member * cols, cols, 0)
     scaled = gain_own[:, None] * image_norm
+    scaled = lax.optimization_barrier(scaled)
     stats = jnp.stack([squares, jnp.sum(scaled * inputs, axis=0)])
     stats = spread(stats, "y")
     stats = jnp.sum(stats, axis=0) / width
     inv_rms = lax.rsqrt(stats[0] + norm_eps)
-    row_ids = jnp.arange(groups * image_rows, dtype=jnp.int32)
-    owner_match = (row_ids // image_rows)[:, None] == jnp.arange(groups, dtype=jnp.int32)[None, :]
-    counts = jnp.sum(jnp.where(owner_match, image_count[None, :], 0), axis=1)
-    live = row_ids % image_rows // PATCH < counts
     image_grad = inv_rms[None, :] * scaled - inputs * (inv_rms**3 * stats[1])[None, :]
     grad_scale = 1.0 / jnp.sqrt(f32(shards * groups * image_rows))
     image_grad = jnp.where(live[None, :], image_grad * grad_scale, 0.0).astype(bf16)
@@ -123,8 +125,7 @@
     other = swapped(other)
     part = dot(vision[:, :half], image_grad, 0, 1) + other.astype(f32)
     part = summed(part.reshape(nx, nz * per_shard, cols), "x")
-    part = summed(part.reshape(nz, per_shard, cols), "z")
-    proj_grad = part.reshape(proj_flat.shape)
+    proj_grad = summed(part.reshape(nz, *proj_flat.shape), "z")
 
     text_in = text_embeds.astype(f32)
     text_rms = lax.rsqrt(jnp.mean(text_in * text_in, axis=-1, keepdims=True) + norm_eps)

time: 189 us -> 174 us (0.921)
  the two profiles are of different devices: /device:TPU:64 before, /device:TPU:2 now
where the time goes in v4:
time: 174 us
  starting transfers between devices  53.7 us (31%)
  waiting for transfers between devices  43.2 us (25%)
  blocking collectives  34.5 us (20%)
  between operations  14.5 us (8%)
  matrix products  12.3 us (7%)
  other arithmetic  9.18 us (5%)
  local copies, waits for them, and re-layouts  6.18 us (4%)
    all_to_all x2, blocking collectives, summed(): lax.all_to_all(blocks.astype(bf16), axis, split_axis=0, concat_axis=0, ti...  34.5 us
    ppermute x6, waiting for transfers between devices, shift(): return lax.ppermute(value, axis, [(i, (i + by) % n) for i in range(n)])  33.1 us
    all_to_all x3, starting transfers between devices, spread(): return lax.all_to_all(copies, axis, split_axis=0, concat_axis=0, tiled=True)  26.5 us
    ppermute x6, starting transfers between devices, shift(): return lax.ppermute(value, axis, [(i, (i + by) % n) for i in range(n)])  23.3 us
    dot_general x6, matrix products, dot(): lax.dot_general(left, right, (((left_dim,), (right_dim,)), ((), ())), pre...  12.3 us
    all_to_all x3, waiting for transfers between devices, spread(): return lax.all_to_all(copies, axis, split_axis=0, concat_axis=0, tiled=True)  8.15 us
    ppermute x2, starting transfers between devices, swapped(): return lax.ppermute(block, 'c', [(0, 1), (1, 0)])  3.84 us
  transfers between devices with their start and end apart: 12, of which 5 were waited for; matrix products, arithmetic and copies ran while one was open for 7% of the time, Pallas kernels for 0%

profile of v4, /device:TPU:2, one launch (start us, length us, event | category | flops | bytes accessed | tf_op | source)
XLA Modules:
  0.0 173.6 jit_solution(7463090125146756571)
XLA Ops:
  7.2 0.0 copy-start
  7.2 0.0 reduce-scatter.2.cloned.1.call-start
  7.2 1.0 slice.40
  8.2 1.2 slice.41
  9.5 3.6 %convolution_convert_fusion.1 = bf16[4096,256]{1,0:T(8,128)(2,1)S(1)} fusion(bf16[4096,512]{1,0:T(8,128)(2,1)} %param.12, bf16[256,512]{1,0:T(8,128)(2,1)S(1)} %bitcast.24), kind=kOutput, calls=%fused_computation.1 | convolution fusion | flops 1074790400 | bytes 6553600 | tf_op jit(solution)/shard_map/dot_general | solution.py:19
  13.1 5.4 %convolution_convert_fusion = bf16[768,4096]{1,0:T(8,128)(2,1)} fusion(bf16[768,512]{1,0:T(8,128)(2,1)S(1)} %bitcast.21, bf16[4096,512]{1,0:T(8,128)(2,1)S(1)} %copy-done.9), kind=kOutput, calls=%fused_computation | convolution fusion | flops 3224371200 | bytes 11272192 | tf_op jit(solution)/shard_map/dot_general | solution.py:19
  18.4 0.0 reduce-scatter.2.cloned.1.call-update
  18.5 0.7 copy-done.7
  19.2 0.7 broadcast_in_dim.31
  19.8 15.2 %all-to-all-start = ((bf16[12,48,128]{2,1,0:T(8,128)(2,1)}), bf16[12,48,128]{2,1,0:T(8,128)(2,1)S(1)}, u32[]{:S(2)}, u32[]{:S(2)}) async-start(bf16[12,48,128]{2,1,0:T(8,128)(2,1)} %broadcast_in_dim.31), calls=%async_computation.1 | async-start | bytes 294912 | tf_op jit(solution)/shard_map/all_to_all | solution.py:27
  35.1 0.1 constant_dynamic-slice_fusion.5
  35.2 0.9 pad_maximum_fusion.1
  36.1 5.4 %collective-permute-start.2 = (bf16[1024,256]{1,0:T(8,128)(2,1)}, bf16[1024,256]{1,0:T(8,128)(2,1)S(1)}, u32[]{:S(2)}, u32[]{:S(2)}) collective-permute-start(bf16[1024,256]{1,0:T(8,128)(2,1)} %pad_maximum_fusion.1), channel_id=1, source_target_pairs={{0,7},{1,0},{2,1},{3,2},{4,3},{5,4},{6,5},{7,6},{8,15},{9,8},{10,9... | collective-permute-start | bytes 1572872 | tf_op jit(solution)/shard_map/ppermute | solution.py:41
  41.4 0.8 pad_maximum_fusion
  42.3 2.0 %collective-permute-start.1 = (bf16[1024,256]{1,0:T(8,128)(2,1)}, bf16[1024,256]{1,0:T(8,128)(2,1)}, u32[]{:S(2)}, u32[]{:S(2)}) collective-permute-start(bf16[1024,256]{1,0:T(8,128)(2,1)} %pad_maximum_fusion), channel_id=1, source_target_pairs={{0,1},{1,2},{2,3},{3,4},{4,5},{5,6},{6,7},{7,0},{8,9},{9,10},{10,1... | collective-permute-start | bytes 1572872 | tf_op jit(solution)/shard_map/ppermute | solution.py:41
  44.3 0.7 constant_dynamic-slice_fusion.1
  45.1 3.0 %collective-permute-start.3 = (bf16[256,256]{1,0:T(8,128)(2,1)}, bf16[256,256]{1,0:T(8,128)(2,1)}, u32[]{:S(2)}, u32[]{:S(2)}) collective-permute-start(bf16[256,256]{1,0:T(8,128)(2,1)} %get-tuple-element.12), channel_id=1, source_target_pairs={{0,2},{1,3},{2,4},{3,5},{4,6},{5,7},{6,0},{7,1},{8,10},{9,11},{10,... | collective-permute-start | bytes 393224 | tf_op jit(solution)/shard_map/ppermute | solution.py:41
  48.1 4.9 %collective-permute-start.5 = (bf16[256,256]{1,0:T(8,128)(2,1)}, bf16[256,256]{1,0:T(8,128)(2,1)}, u32[]{:S(2)}, u32[]{:S(2)}) collective-permute-start(bf16[256,256]{1,0:T(8,128)(2,1)} %get-tuple-element.13), channel_id=1, source_target_pairs={{0,6},{1,7},{2,0},{3,1},{4,2},{5,3},{6,4},{7,5},{8,14},{9,15},{10,... | collective-permute-start | bytes 393224 | tf_op jit(solution)/shard_map/ppermute | solution.py:41
  53.0 0.1 broadcast_in_dim.32
  53.2 0.9 broadcast_in_dim.37
  54.0 5.0 %all-to-all-start.1 = ((bf16[4,144,512]{2,1,0:T(8,128)(2,1)}), bf16[4,144,512]{2,1,0:T(8,128)(2,1)}, u32[]{:S(2)}, u32[]{:S(2)}) async-start(bf16[4,144,512]{2,1,0:T(8,128)(2,1)} %broadcast_in_dim.37), calls=%async_computation.2 | async-start | bytes 1179648 | tf_op jit(solution)/shard_map/all_to_all | solution.py:27
  59.0 0.1 select_reduce_fusion
  59.1 19.9 %collective-permute-done.3 = bf16[256,256]{1,0:T(8,128)(2,1)} collective-permute-done((bf16[256,256]{1,0:T(8,128)(2,1)}, bf16[256,256]{1,0:T(8,128)(2,1)}, u32[]{:S(2)}, u32[]{:S(2)}) %collective-permute-start.3) | collective-permute-done | bytes 131104 | tf_op jit(solution)/shard_map/ppermute | solution.py:41
  79.0 2.1 %add_convert_fusion.2 = (bf16[512,256]{1,0:T(8,128)(2,1)}, bf16[512,256]{1,0:T(8,128)(2,1)S(1)}) fusion(bf16[1024,256]{1,0:T(8,128)(2,1)} %collective-permute-done.1, bf16[4096,256]{1,0:T(8,128)(2,1)S(1)} %convolution_convert_fusion.1, s32[]{:T(128)S(6)} %select_n.183, bf16[256,256]{1,0:T(8,128)(2,1)} %collective-permute-done.3, ...), kind=kLoop, calls=%fused_computation.28 | loop fusion | flops 1572864 | bytes 1835016 | tf_op jit(solution)/shard_map/convert_element_type | solution.py:59
  81.1 1.9 %collective-permute-start.4 = (bf16[512,256]{1,0:T(8,128)(2,1)}, bf16[512,256]{1,0:T(8,128)(2,1)}, u32[]{:S(2)}, u32[]{:S(2)}) collective-permute-start(bf16[512,256]{1,0:T(8,128)(2,1)} %get-tuple-element.10), channel_id=1, source_target_pairs={{0,2},{1,3},{2,4},{3,5},{4,6},{5,7},{6,0},{7,1},{8,10},{9,11},{10,... | collective-permute-start | bytes 786440 | tf_op jit(solution)/shard_map/ppermute | solution.py:41
  83.0 6.0 %collective-permute-start.6 = (bf16[512,256]{1,0:T(8,128)(2,1)S(1)}, bf16[512,256]{1,0:T(8,128)(2,1)}, u32[]{:S(2)}, u32[]{:S(2)}) collective-permute-start(bf16[512,256]{1,0:T(8,128)(2,1)S(1)} %get-tuple-element.11), channel_id=1, source_target_pairs={{0,6},{1,7},{2,0},{3,1},{4,2},{5,3},{6,4},{7,5},{8,14},{9,15},{10,... | collective-permute-start | bytes 786440 | tf_op jit(solution)/shard_map/ppermute | solution.py:41
  89.1 1.9 %collective-permute-start = (bf16[576,512]{1,0:T(8,128)(2,1)}, bf16[576,512]{1,0:T(8,128)(2,1)}, u32[]{:S(2)}, u32[]{:S(2)}) collective-permute-start(bf16[576,512]{1,0:T(8,128)(2,1)} %bitcast.4), channel_id=1, source_target_pairs={{0,8},{8,0},{1,9},{9,1},{2,10},{10,2},{3,11},{11,3},{4,12},{12,4},... | collective-permute-start | bytes 1769480 | tf_op jit(solution)/shard_map/ppermute | solution.py:36
  91.1 0.1 dynamic_slice.30
  91.1 0.8 convolution_convert_fusion.2
  92.0 12.3 %collective-permute-done.4 = bf16[512,256]{1,0:T(8,128)(2,1)} collective-permute-done((bf16[512,256]{1,0:T(8,128)(2,1)}, bf16[512,256]{1,0:T(8,128)(2,1)}, u32[]{:S(2)}, u32[]{:S(2)}) %collective-permute-start.4) | collective-permute-done | bytes 262176 | tf_op jit(solution)/shard_map/ppermute | solution.py:41
  104.3 0.9 collective-permute-done.6
  105.2 1.4 add_multiply_fusion
  106.5 1.8 %multiply_reduce_fusion.1 = (f32[256]{0:T(256)S(1)}, f32[256]{0:T(256)S(1)}, f32[512,256]{1,0:T(8,128)S(1)}) fusion(f32[512,256]{1,0:T(8,128)S(1)} %add_multiply_fusion, bf16[1152,256]{1,0:T(8,128)(2,1)S(1)} %convolution_convert_fusion.2, bf16[576,512]{1,0:T(8,128)(2,1)} %collective-permute-done, bf16[576,512]{1,0:T(8,128)(2,1)} %bitcast.4), kind=kOutput, calls=%fused_computation.29 | convolution fusion | flops 305135104 | bytes 2820096 | tf_op jit(solution)/shard_map/dot_general | solution.py:19
  108.4 0.6 broadcast_in_dim.38
  109.0 6.4 %all-to-all-start.2 = ((f32[8,2,256]{2,1,0:T(2,128)}), f32[8,2,256]{2,1,0:T(2,128)S(1)}, u32[]{:S(2)}, u32[]{:S(2)}) async-start(f32[8,2,256]{2,1,0:T(2,128)} %broadcast_in_dim.38), calls=%async_computation.3 | async-start | bytes 32768 | tf_op jit(solution)/shard_map/all_to_all | solution.py:27
  115.4 8.1 %all-to-all-done.2 = f32[8,2,256]{2,1,0:T(2,128)S(1)} async-done(((f32[8,2,256]{2,1,0:T(2,128)}), f32[8,2,256]{2,1,0:T(2,128)S(1)}, u32[]{:S(2)}, u32[]{:S(2)}) %all-to-all-start.2) | async-done | bytes 16416 | tf_op jit(solution)/shard_map/all_to_all | solution.py:27
  123.6 0.1 select_convert_fusion
  123.7 0.3 convolution_convert_fusion.3
  124.1 1.9 %collective-permute-start.7 = (bf16[576,512]{1,0:T(8,128)(2,1)S(1)}, bf16[576,512]{1,0:T(8,128)(2,1)S(1)}, u32[]{:S(2)}, u32[]{:S(2)}) collective-permute-start(bf16[576,512]{1,0:T(8,128)(2,1)S(1)} %convolution_convert_fusion.3), channel_id=1, source_target_pairs={{0,8},{8,0},{1,9},{9,1},{2,10},{10,2},{3,11},{11,3},{4,12},{12,4},... | collective-permute-start | bytes 1769480 | tf_op jit(solution)/shard_map/ppermute | solution.py:36
  126.0 2.0 %collective-permute-done.7 = bf16[576,512]{1,0:T(8,128)(2,1)S(1)} collective-permute-done((bf16[576,512]{1,0:T(8,128)(2,1)S(1)}, bf16[576,512]{1,0:T(8,128)(2,1)S(1)}, u32[]{:S(2)}, u32[]{:S(2)}) %collective-permute-start.7) | collective-permute-done | bytes 589856 | tf_op jit(solution)/shard_map/ppermute | solution.py:36
  128.0 0.3 add_convert_fusion
  128.4 13.8 %all_to_all.25 = bf16[4,144,512]{2,1,0:T(8,128)(2,1)S(1)} all-to-all(bf16[4,144,512]{2,1,0:T(8,128)(2,1)S(1)} %bitcast.18), channel_id=1, replica_groups=mesh['z'=12,'x'=4,'c'=2,'y'=8] {'x'}, dimensions={0} | all-to-all | bytes 1179648 | tf_op jit(solution)/shard_map/all_to_all | solution.py:31
  142.1 0.1 reduce_sum.81
  142.2 0.1 convert_element_type.112
  142.3 20.7 %all_to_all.26 = bf16[12,48,128]{2,1,0:T(8,128)(2,1)S(1)} all-to-all(bf16[12,48,128]{2,1,0:T(8,128)(2,1)S(1)} %convert_element_type.112), channel_id=1, replica_groups=mesh['z'=12,'x'=4,'c'=2,'y'=8] {'z'}, dimensions={0} | all-to-all | bytes 294912 | tf_op jit(solution)/shard_map/all_to_all | solution.py:31
  163.1 0.6 convert_reduce_fusion
  163.7 1.7 fusion.3
  165.4 1.3 fusion.6
  (34 shorter events, 0.2 us)
Async XLA Ops:
  7.2 84.0 %copy-start = (bf16[256,1024]{1,0:T(8,128)(2,1)S(1)}, bf16[256,1024]{1,0:T(8,128)(2,1)}, u32[]{:S(2)}) copy-start(bf16[256,1024]{1,0:T(8,128)(2,1)} %param.7) | copy-start | bytes 1572868
  7.2 156.5 %reduce-scatter.2.cloned.1.call-start = ((), (), s32[]{:S(2)}) async-start(), calls=%async_computation.6 | async-start | bytes 7077888 | tf_op jit(solution)/shard_map/reduce_scatter | solution.py:95
  9.4 3.6 %copy-start.9 = (bf16[4096,512]{1,0:T(8,128)(2,1)S(1)}, bf16[4096,512]{1,0:T(8,128)(2,1)}, u32[]{:S(2)}) copy-start(bf16[4096,512]{1,0:T(8,128)(2,1)} %param.12) | copy-start | bytes 12582916
  18.4 0.7 copy-start.7
  19.8 33.2 %all-to-all-start = ((bf16[12,48,128]{2,1,0:T(8,128)(2,1)}), bf16[12,48,128]{2,1,0:T(8,128)(2,1)S(1)}, u32[]{:S(2)}, u32[]{:S(2)}) async-start(bf16[12,48,128]{2,1,0:T(8,128)(2,1)} %broadcast_in_dim.31), calls=%async_computation.1 | async-start | bytes 294912 | tf_op jit(solution)/shard_map/all_to_all | solution.py:27
  36.1 42.9 %collective-permute-start.2 = (bf16[1024,256]{1,0:T(8,128)(2,1)}, bf16[1024,256]{1,0:T(8,128)(2,1)S(1)}, u32[]{:S(2)}, u32[]{:S(2)}) collective-permute-start(bf16[1024,256]{1,0:T(8,128)(2,1)} %pad_maximum_fusion.1), channel_id=1, source_target_pairs={{0,7},{1,0},{2,1},{3,2},{4,3},{5,4},{6,5},{7,6},{8,15},{9,8},{10,9... | collective-permute-start | bytes 1572872 | tf_op jit(solution)/shard_map/ppermute | solution.py:41
  42.3 16.7 %copy-start.8 = (s32[8]{0:T(128)S(1)}, s32[8]{0:T(128)}, u32[]{:S(2)}) copy-start(s32[8]{0:T(128)} %param.8) | copy-start | bytes 100
  42.3 36.7 %collective-permute-start.1 = (bf16[1024,256]{1,0:T(8,128)(2,1)}, bf16[1024,256]{1,0:T(8,128)(2,1)}, u32[]{:S(2)}, u32[]{:S(2)}) collective-permute-start(bf16[1024,256]{1,0:T(8,128)(2,1)} %pad_maximum_fusion), channel_id=1, source_target_pairs={{0,1},{1,2},{2,3},{3,4},{4,5},{5,6},{6,7},{7,0},{8,9},{9,10},{10,1... | collective-permute-start | bytes 1572872 | tf_op jit(solution)/shard_map/ppermute | solution.py:41
  45.1 33.9 %collective-permute-start.3 = (bf16[256,256]{1,0:T(8,128)(2,1)}, bf16[256,256]{1,0:T(8,128)(2,1)}, u32[]{:S(2)}, u32[]{:S(2)}) collective-permute-start(bf16[256,256]{1,0:T(8,128)(2,1)} %get-tuple-element.12), channel_id=1, source_target_pairs={{0,2},{1,3},{2,4},{3,5},{4,6},{5,7},{6,0},{7,1},{8,10},{9,11},{10,... | collective-permute-start | bytes 393224 | tf_op jit(solution)/shard_map/ppermute | solution.py:41
  48.1 30.9 %collective-permute-start.5 = (bf16[256,256]{1,0:T(8,128)(2,1)}, bf16[256,256]{1,0:T(8,128)(2,1)}, u32[]{:S(2)}, u32[]{:S(2)}) collective-permute-start(bf16[256,256]{1,0:T(8,128)(2,1)} %get-tuple-element.13), channel_id=1, source_target_pairs={{0,6},{1,7},{2,0},{3,1},{4,2},{5,3},{6,4},{7,5},{8,14},{9,15},{10,... | collective-permute-start | bytes 393224 | tf_op jit(solution)/shard_map/ppermute | solution.py:41
  54.0 37.0 %copy-start.6 = (f32[4096]{0:T(1024)S(1)}, f32[4096]{0:T(1024)}, u32[]{:S(2)}) copy-start(f32[4096]{0:T(1024)} %param.11) | copy-start | bytes 49156
  54.0 35.0 %all-to-all-start.1 = ((bf16[4,144,512]{2,1,0:T(8,128)(2,1)}), bf16[4,144,512]{2,1,0:T(8,128)(2,1)}, u32[]{:S(2)}, u32[]{:S(2)}) async-start(bf16[4,144,512]{2,1,0:T(8,128)(2,1)} %broadcast_in_dim.37), calls=%async_computation.2 | async-start | bytes 1179648 | tf_op jit(solution)/shard_map/all_to_all | solution.py:27
  79.0 13.0 %copy-start.5 = (bf16[1024,256]{1,0:T(8,128)(2,1)}, bf16[1024,256]{1,0:T(8,128)(2,1)S(1)}, u32[]{:S(2)}) copy-start(bf16[1024,256]{1,0:T(8,128)(2,1)S(1)} %collective-permute-done.2) | copy-start | bytes 1572868
  81.1 23.2 %collective-permute-start.4 = (bf16[512,256]{1,0:T(8,128)(2,1)}, bf16[512,256]{1,0:T(8,128)(2,1)}, u32[]{:S(2)}, u32[]{:S(2)}) collective-permute-start(bf16[512,256]{1,0:T(8,128)(2,1)} %get-tuple-element.10), channel_id=1, source_target_pairs={{0,2},{1,3},{2,4},{3,5},{4,6},{5,7},{6,0},{7,1},{8,10},{9,11},{10,... | collective-permute-start | bytes 786440 | tf_op jit(solution)/shard_map/ppermute | solution.py:41
  83.0 22.1 %collective-permute-start.6 = (bf16[512,256]{1,0:T(8,128)(2,1)S(1)}, bf16[512,256]{1,0:T(8,128)(2,1)}, u32[]{:S(2)}, u32[]{:S(2)}) collective-permute-start(bf16[512,256]{1,0:T(8,128)(2,1)S(1)} %get-tuple-element.11), channel_id=1, source_target_pairs={{0,6},{1,7},{2,0},{3,1},{4,2},{5,3},{6,4},{7,5},{8,14},{9,15},{10,... | collective-permute-start | bytes 786440 | tf_op jit(solution)/shard_map/ppermute | solution.py:41
  89.1 17.5 %collective-permute-start = (bf16[576,512]{1,0:T(8,128)(2,1)}, bf16[576,512]{1,0:T(8,128)(2,1)}, u32[]{:S(2)}, u32[]{:S(2)}) collective-permute-start(bf16[576,512]{1,0:T(8,128)(2,1)} %bitcast.4), channel_id=1, source_target_pairs={{0,8},{8,0},{1,9},{9,1},{2,10},{10,2},{3,11},{11,3},{4,12},{12,4},... | collective-permute-start | bytes 1769480 | tf_op jit(solution)/shard_map/ppermute | solution.py:36
  92.0 16.4 %copy-start.3 = (bf16[1152,256]{1,0:T(8,128)(2,1)}, bf16[1152,256]{1,0:T(8,128)(2,1)S(1)}, u32[]{:S(2)}) copy-start(bf16[1152,256]{1,0:T(8,128)(2,1)S(1)} %convolution_convert_fusion.2) | copy-start | bytes 1769476
  108.4 15.4 %copy-start.4 = (bf16[1152,256]{1,0:T(8,128)(2,1)S(1)}, bf16[1152,256]{1,0:T(8,128)(2,1)}, u32[]{:S(2)}) copy-start(bf16[1152,256]{1,0:T(8,128)(2,1)} %copy-done.3) | copy-start | bytes 1769476
  109.0 14.6 %all-to-all-start.2 = ((f32[8,2,256]{2,1,0:T(2,128)}), f32[8,2,256]{2,1,0:T(2,128)S(1)}, u32[]{:S(2)}, u32[]{:S(2)}) async-start(f32[8,2,256]{2,1,0:T(2,128)} %broadcast_in_dim.38), calls=%async_computation.3 | async-start | bytes 32768 | tf_op jit(solution)/shard_map/all_to_all | solution.py:27
  124.1 3.9 %collective-permute-start.7 = (bf16[576,512]{1,0:T(8,128)(2,1)S(1)}, bf16[576,512]{1,0:T(8,128)(2,1)S(1)}, u32[]{:S(2)}, u32[]{:S(2)}) collective-permute-start(bf16[576,512]{1,0:T(8,128)(2,1)S(1)} %convolution_convert_fusion.3), channel_id=1, source_target_pairs={{0,8},{8,0},{1,9},{9,1},{2,10},{10,2},{3,11},{11,3},{4,12},{12,4},... | collective-permute-start | bytes 1769480 | tf_op jit(solution)/shard_map/ppermute | solution.py:36
  128.3 35.3 %copy-start.1 = (bf16[96,4096]{1,0:T(8,128)(2,1)S(1)}, bf16[96,4096]{1,0:T(8,128)(2,1)}, u32[]{:S(2)}) copy-start(bf16[96,4096]{1,0:T(8,128)(2,1)} %param.10) | copy-start | bytes 2359300
  163.7 1.7 copy-start.2
Sparse Core Ops, SparseCore 0:
  18.6 115.3 reduce-scatter.1

commit v5 on v4

--- a/solution.py
+++ b/solution.py
@@ -58,6 +58,7 @@
     up = jnp.concatenate([far_up.astype(f32), rest], axis=0)
     up = (up + chunk(2).astype(f32) + near_up[:size].astype(f32)).astype(part.dtype)
     up = shift(up, axis, 2)
+    far_down, near_down, part = lax.optimization_barrier((far_down, near_down, part))
     down = jnp.concatenate([rest, far_down.astype(f32)], axis=0)
     down = (down + chunk(-2).astype(f32) + near_down[:size].astype(f32)).astype(part.dtype)
     down = shift(down, axis, -2)
@@ -83,7 +84,7 @@
     rows = rows.reshape(nz * per_shard, cols)
     rows = spread(rows, "x")
     rows = rows.reshape(half, cols)
-    proj = jnp.concatenate([rows, swapped(rows)], axis=0)
+    other_rows = swapped(rows)
 
     q_own = q_grad.reshape(groups, own_rows, cols)
     q_image = q_own[:, :image_rows].reshape(groups * image_rows, cols)
@@ -102,7 +103,9 @@
     source = ((zi * nx + xi) * nc + ci) * per_shard + row
     pick = (jnp.arange(enc, dtype=jnp.int32)[:, None] == source[None, :]).astype(bf16)
     vision = dot(vision_rows, pick, 1, 0).astype(bf16)
-    embed = dot(proj, vision, 0, 1).astype(bf16)
+    embed_own = dot(rows, vision[:, :half], 0, 1)
+    embed_own = lax.optimization_barrier(embed_own)
+    embed = (embed_own + dot(other_rows, vision[:, half:], 0, 1)).astype(bf16)
     squares = jnp.sum(jnp.square(embed.astype(f32)), axis=0)
     inputs = embed.astype(f32)
 

time: 174 us -> 167 us (0.960)
  starting transfers between devices: 53.7 us -> 48.2 us
    ppermute x6, starting transfers between devices: 23.3 us -> 20.1 us  [shift(): return lax.ppermute(value, axis, [(i, (i + by) % n) for i in range(n)])]
    all_to_all x3, starting transfers between devices: 26.5 us -> 24.2 us  [spread(): return lax.all_to_all(copies, axis, split_axis=0, concat_axis=0, tiled=True)]
    all_to_all x3, waiting for transfers between devices: 8.15 us -> 10.5 us  [spread(): return lax.all_to_all(copies, axis, split_axis=0, concat_axis=0, tiled=True)]
    dot_general x6 -> x7, matrix products: 12.3 us -> 11.3 us  [dot(): lax.dot_general(left, right, (((left_dim,), (right_dim,)), ((), ())), pre...]
where the time goes in v5:
time: 167 us
  starting transfers between devices  48.2 us (29%)
  waiting for transfers between devices  44 us (26%)
  blocking collectives  34.1 us (20%)
  between operations  14.5 us (9%)
  matrix products  11.3 us (7%)
  other arithmetic  9.63 us (6%)
  local copies, waits for them, and re-layouts  4.8 us (3%)
    all_to_all x2, blocking collectives, summed(): lax.all_to_all(blocks.astype(bf16), axis, split_axis=0, concat_axis=0, ti...  34.1 us
    ppermute x6, waiting for transfers between devices, shift(): return lax.ppermute(value, axis, [(i, (i + by) % n) for i in range(n)])  31.5 us
    all_to_all x3, starting transfers between devices, spread(): return lax.all_to_all(copies, axis, split_axis=0, concat_axis=0, tiled=True)  24.2 us
    ppermute x6, starting transfers between devices, shift(): return lax.ppermute(value, axis, [(i, (i + by) % n) for i in range(n)])  20.1 us
    dot_general x7, matrix products, dot(): lax.dot_general(left, right, (((left_dim,), (right_dim,)), ((), ())), pre...  11.3 us
    all_to_all x3, waiting for transfers between devices, spread(): return lax.all_to_all(copies, axis, split_axis=0, concat_axis=0, tiled=True)  10.5 us
    ppermute x2, starting transfers between devices, swapped(): return lax.ppermute(block, 'c', [(0, 1), (1, 0)])  3.83 us
  transfers between devices with their start and end apart: 12, of which 5 were waited for; matrix products, arithmetic and copies ran while one was open for 7% of the time, Pallas kernels for 0%

profile of v5, /device:TPU:2, one launch (start us, length us, event | category | flops | bytes accessed | tf_op | source)
XLA Modules:
  0.0 166.6 jit_solution(5207405620300191229)
XLA Ops:
  7.2 0.0 reduce-scatter.2.cloned.1.call-start
  7.2 1.0 slice.42
  8.2 1.2 slice.43
  9.5 3.6 %convolution_convert_fusion.1 = bf16[4096,256]{1,0:T(8,128)(2,1)S(1)} fusion(bf16[4096,512]{1,0:T(8,128)(2,1)} %param.12, bf16[256,512]{1,0:T(8,128)(2,1)S(1)} %bitcast.36), kind=kOutput, calls=%fused_computation.1 | convolution fusion | flops 1074790400 | bytes 6553600 | tf_op jit(solution)/shard_map/dot_general | solution.py:19
  13.1 5.3 %convolution_convert_fusion = bf16[768,4096]{1,0:T(8,128)(2,1)} fusion(bf16[768,512]{1,0:T(8,128)(2,1)S(1)} %bitcast.35, bf16[4096,512]{1,0:T(8,128)(2,1)S(1)} %copy-done.8), kind=kOutput, calls=%fused_computation | convolution fusion | flops 3224371200 | bytes 11272192 | tf_op jit(solution)/shard_map/dot_general | solution.py:19
  18.4 0.0 reduce-scatter.2.cloned.1.call-update
  18.5 0.1 constant_dynamic-slice_fusion.2
  18.6 0.8 pad_maximum_fusion
  19.5 5.4 %collective-permute-start.2 = (bf16[1024,256]{1,0:T(8,128)(2,1)}, bf16[1024,256]{1,0:T(8,128)(2,1)}, u32[]{:S(2)}, u32[]{:S(2)}) collective-permute-start(bf16[1024,256]{1,0:T(8,128)(2,1)} %pad_maximum_fusion), channel_id=1, source_target_pairs={{0,7},{1,0},{2,1},{3,2},{4,3},{5,4},{6,5},{7,6},{8,15},{9,8},{10,9... | collective-permute-start | bytes 1572872 | tf_op jit(solution)/shard_map/ppermute | solution.py:41
  24.8 0.7 broadcast_in_dim.31
  25.5 15.2 %all-to-all-start = ((bf16[12,48,128]{2,1,0:T(8,128)(2,1)}), bf16[12,48,128]{2,1,0:T(8,128)(2,1)S(1)}, u32[]{:S(2)}, u32[]{:S(2)}) async-start(bf16[12,48,128]{2,1,0:T(8,128)(2,1)} %broadcast_in_dim.31), calls=%async_computation.1 | async-start | bytes 294912 | tf_op jit(solution)/shard_map/all_to_all | solution.py:27
  40.7 0.9 pad_maximum_fusion.1
  41.5 1.9 %collective-permute-start.3 = (bf16[1024,256]{1,0:T(8,128)(2,1)}, bf16[1024,256]{1,0:T(8,128)(2,1)S(1)}, u32[]{:S(2)}, u32[]{:S(2)}) collective-permute-start(bf16[1024,256]{1,0:T(8,128)(2,1)} %pad_maximum_fusion.1), channel_id=1, source_target_pairs={{0,1},{1,2},{2,3},{3,4},{4,5},{5,6},{6,7},{7,0},{8,9},{9,10},{10,1... | collective-permute-start | bytes 1572872 | tf_op jit(solution)/shard_map/ppermute | solution.py:41
  43.5 4.7 %collective-permute-start.1 = (bf16[256,256]{1,0:T(8,128)(2,1)S(1)}, bf16[256,256]{1,0:T(8,128)(2,1)S(1)}, u32[]{:S(2)}, u32[]{:S(2)}) collective-permute-start(bf16[256,256]{1,0:T(8,128)(2,1)S(1)} %get-tuple-element.17), channel_id=1, source_target_pairs={{0,6},{1,7},{2,0},{3,1},{4,2},{5,3},{6,4},{7,5},{8,14},{9,15},{10,... | collective-permute-start | bytes 393224 | tf_op jit(solution)/shard_map/ppermute | solution.py:41
  48.2 2.0 %collective-permute-start.4 = (bf16[256,256]{1,0:T(8,128)(2,1)S(1)}, bf16[256,256]{1,0:T(8,128)(2,1)S(1)}, u32[]{:S(2)}, u32[]{:S(2)}) collective-permute-start(bf16[256,256]{1,0:T(8,128)(2,1)S(1)} %get-tuple-element.16), channel_id=1, source_target_pairs={{0,2},{1,3},{2,4},{3,5},{4,6},{5,7},{6,0},{7,1},{8,10},{9,11},{10,... | collective-permute-start | bytes 393224 | tf_op jit(solution)/shard_map/ppermute | solution.py:41
  50.3 0.6 fusion.32
  50.9 2.3 %all-to-all-done = bf16[12,48,128]{2,1,0:T(8,128)(2,1)S(1)} async-done(((bf16[12,48,128]{2,1,0:T(8,128)(2,1)}), bf16[12,48,128]{2,1,0:T(8,128)(2,1)S(1)}, u32[]{:S(2)}, u32[]{:S(2)}) %all-to-all-start) | async-done | bytes 147488 | tf_op jit(solution)/shard_map/all_to_all | solution.py:27
  53.3 0.1 broadcast_in_dim.32
  53.4 0.9 broadcast_in_dim.37
  54.2 4.8 %all-to-all-start.1 = ((bf16[4,144,512]{2,1,0:T(8,128)(2,1)}), bf16[4,144,512]{2,1,0:T(8,128)(2,1)S(1)}, u32[]{:S(2)}, u32[]{:S(2)}) async-start(bf16[4,144,512]{2,1,0:T(8,128)(2,1)} %broadcast_in_dim.37), calls=%async_computation.2 | async-start | bytes 1179648 | tf_op jit(solution)/shard_map/all_to_all | solution.py:27
  59.1 1.1 add_convert_fusion.1
  60.2 4.2 %collective-permute-start.6 = (bf16[512,256]{1,0:T(8,128)(2,1)S(1)}, bf16[512,256]{1,0:T(8,128)(2,1)S(1)}, u32[]{:S(2)}, u32[]{:S(2)}) collective-permute-start(bf16[512,256]{1,0:T(8,128)(2,1)S(1)} %add_convert_fusion.1), channel_id=1, source_target_pairs={{0,6},{1,7},{2,0},{3,1},{4,2},{5,3},{6,4},{7,5},{8,14},{9,15},{10,... | collective-permute-start | bytes 786440 | tf_op jit(solution)/shard_map/ppermute | solution.py:41
  64.4 13.6 %collective-permute-done.4 = bf16[256,256]{1,0:T(8,128)(2,1)S(1)} collective-permute-done((bf16[256,256]{1,0:T(8,128)(2,1)S(1)}, bf16[256,256]{1,0:T(8,128)(2,1)S(1)}, u32[]{:S(2)}, u32[]{:S(2)}) %collective-permute-start.4) | collective-permute-done | bytes 131104 | tf_op jit(solution)/shard_map/ppermute | solution.py:41
  78.0 1.0 add_convert_fusion.2
  79.1 1.9 %collective-permute-start.5 = (bf16[512,256]{1,0:T(8,128)(2,1)S(1)}, bf16[512,256]{1,0:T(8,128)(2,1)S(1)}, u32[]{:S(2)}, u32[]{:S(2)}) collective-permute-start(bf16[512,256]{1,0:T(8,128)(2,1)S(1)} %add_convert_fusion.2), channel_id=1, source_target_pairs={{0,2},{1,3},{2,4},{3,5},{4,6},{5,7},{6,0},{7,1},{8,10},{9,11},{10,... | collective-permute-start | bytes 786440 | tf_op jit(solution)/shard_map/ppermute | solution.py:41
  81.0 0.8 fusion.1
  81.9 0.1 dynamic_slice.30
  82.0 1.9 %collective-permute-start = (bf16[576,512]{1,0:T(8,128)(2,1)S(1)}, bf16[576,512]{1,0:T(8,128)(2,1)S(1)}, u32[]{:S(2)}, u32[]{:S(2)}) collective-permute-start(bf16[576,512]{1,0:T(8,128)(2,1)S(1)} %bitcast.31), channel_id=1, source_target_pairs={{0,8},{8,0},{1,9},{9,1},{2,10},{10,2},{3,11},{11,3},{4,12},{12,4},... | collective-permute-start | bytes 1769480 | tf_op jit(solution)/shard_map/ppermute | solution.py:36
  83.9 0.1 select_reduce_fusion
  84.0 17.9 %collective-permute-done.5 = bf16[512,256]{1,0:T(8,128)(2,1)S(1)} collective-permute-done((bf16[512,256]{1,0:T(8,128)(2,1)S(1)}, bf16[512,256]{1,0:T(8,128)(2,1)S(1)}, u32[]{:S(2)}, u32[]{:S(2)}) %collective-permute-start.5) | collective-permute-done | bytes 262176 | tf_op jit(solution)/shard_map/ppermute | solution.py:41
  101.9 1.2 add_multiply_fusion
  103.1 0.4 convolution_bitcast_fusion.1
  103.5 0.4 multiply_reduce_fusion.1
  104.0 0.6 broadcast_in_dim.38
  104.6 4.2 %all-to-all-start.2 = ((f32[8,2,256]{2,1,0:T(2,128)}), f32[8,2,256]{2,1,0:T(2,128)S(1)}, u32[]{:S(2)}, u32[]{:S(2)}) async-start(f32[8,2,256]{2,1,0:T(2,128)} %broadcast_in_dim.38), calls=%async_computation.3 | async-start | bytes 32768 | tf_op jit(solution)/shard_map/all_to_all | solution.py:27
  108.8 8.1 %all-to-all-done.2 = f32[8,2,256]{2,1,0:T(2,128)S(1)} async-done(((f32[8,2,256]{2,1,0:T(2,128)}), f32[8,2,256]{2,1,0:T(2,128)S(1)}, u32[]{:S(2)}, u32[]{:S(2)}) %all-to-all-start.2) | async-done | bytes 16416 | tf_op jit(solution)/shard_map/all_to_all | solution.py:27
  117.0 0.1 select_convert_fusion
  117.1 0.3 convolution_convert_fusion.3
  117.5 1.9 %collective-permute-start.7 = (bf16[576,512]{1,0:T(8,128)(2,1)S(1)}, bf16[576,512]{1,0:T(8,128)(2,1)S(1)}, u32[]{:S(2)}, u32[]{:S(2)}) collective-permute-start(bf16[576,512]{1,0:T(8,128)(2,1)S(1)} %convolution_convert_fusion.3), channel_id=1, source_target_pairs={{0,8},{8,0},{1,9},{9,1},{2,10},{10,2},{3,11},{11,3},{4,12},{12,4},... | collective-permute-start | bytes 1769480 | tf_op jit(solution)/shard_map/ppermute | solution.py:36
  119.4 2.0 %collective-permute-done.7 = bf16[576,512]{1,0:T(8,128)(2,1)S(1)} collective-permute-done((bf16[576,512]{1,0:T(8,128)(2,1)S(1)}, bf16[576,512]{1,0:T(8,128)(2,1)S(1)}, u32[]{:S(2)}, u32[]{:S(2)}) %collective-permute-start.7) | collective-permute-done | bytes 589856 | tf_op jit(solution)/shard_map/ppermute | solution.py:36
  121.4 0.3 add_convert_fusion
  121.7 13.8 %all_to_all.25 = bf16[4,144,512]{2,1,0:T(8,128)(2,1)S(1)} all-to-all(bf16[4,144,512]{2,1,0:T(8,128)(2,1)S(1)} %bitcast.30), channel_id=1, replica_groups=mesh['z'=12,'x'=4,'c'=2,'y'=8] {'x'}, dimensions={0} | all-to-all | bytes 1179648 | tf_op jit(solution)/shard_map/all_to_all | solution.py:31
  135.6 0.1 reduce_sum.81
  135.7 0.1 convert_element_type.112
  135.8 20.3 %all_to_all.26 = bf16[12,48,128]{2,1,0:T(8,128)(2,1)S(1)} all-to-all(bf16[12,48,128]{2,1,0:T(8,128)(2,1)S(1)} %convert_element_type.112), channel_id=1, replica_groups=mesh['z'=12,'x'=4,'c'=2,'y'=8] {'z'}, dimensions={0} | all-to-all | bytes 294912 | tf_op jit(solution)/shard_map/all_to_all | solution.py:31
  156.0 0.6 convert_reduce_fusion
  156.7 1.7 fusion.4
  158.4 1.3 fusion.7
  (34 shorter events, 0.2 us)
Async XLA Ops:
  7.2 73.8 %copy-start = (bf16[256,1024]{1,0:T(8,128)(2,1)S(1)}, bf16[256,1024]{1,0:T(8,128)(2,1)}, u32[]{:S(2)}) copy-start(bf16[256,1024]{1,0:T(8,128)(2,1)} %param.7) | copy-start | bytes 1572868
  7.2 149.5 %reduce-scatter.2.cloned.1.call-start = ((), (), s32[]{:S(2)}) async-start(), calls=%async_computation.6 | async-start | bytes 7077888 | tf_op jit(solution)/shard_map/reduce_scatter | solution.py:96
  9.4 3.6 %copy-start.8 = (bf16[4096,512]{1,0:T(8,128)(2,1)S(1)}, bf16[4096,512]{1,0:T(8,128)(2,1)}, u32[]{:S(2)}) copy-start(bf16[4096,512]{1,0:T(8,128)(2,1)} %param.12) | copy-start | bytes 12582916
  13.1 30.4 %copy-start.3 = (bf16[4096,256]{1,0:T(8,128)(2,1)}, bf16[4096,256]{1,0:T(8,128)(2,1)S(1)}, u32[]{:S(2)}) copy-start(bf16[4096,256]{1,0:T(8,128)(2,1)S(1)} %convolution_convert_fusion.1) | copy-start | bytes 6291460
  18.5 6.3 %copy-start.5 = (bf16[48,128]{1,0:T(8,128)(2,1)S(1)}, bf16[48,128]{1,0:T(8,128)(2,1)}, u32[]{:S(2)}) copy-start(bf16[48,128]{1,0:T(8,128)(2,1)} %param.9) | copy-start | bytes 36868
  19.5 39.6 %collective-permute-start.2 = (bf16[1024,256]{1,0:T(8,128)(2,1)}, bf16[1024,256]{1,0:T(8,128)(2,1)}, u32[]{:S(2)}, u32[]{:S(2)}) collective-permute-start(bf16[1024,256]{1,0:T(8,128)(2,1)} %pad_maximum_fusion), channel_id=1, source_target_pairs={{0,7},{1,0},{2,1},{3,2},{4,3},{5,4},{6,5},{7,6},{8,15},{9,8},{10,9... | collective-permute-start | bytes 1572872 | tf_op jit(solution)/shard_map/ppermute | solution.py:41
  25.5 27.7 %all-to-all-start = ((bf16[12,48,128]{2,1,0:T(8,128)(2,1)}), bf16[12,48,128]{2,1,0:T(8,128)(2,1)S(1)}, u32[]{:S(2)}, u32[]{:S(2)}) async-start(bf16[12,48,128]{2,1,0:T(8,128)(2,1)} %broadcast_in_dim.31), calls=%async_computation.1 | async-start | bytes 294912 | tf_op jit(solution)/shard_map/all_to_all | solution.py:27
  41.5 36.5 %collective-permute-start.3 = (bf16[1024,256]{1,0:T(8,128)(2,1)}, bf16[1024,256]{1,0:T(8,128)(2,1)S(1)}, u32[]{:S(2)}, u32[]{:S(2)}) collective-permute-start(bf16[1024,256]{1,0:T(8,128)(2,1)} %pad_maximum_fusion.1), channel_id=1, source_target_pairs={{0,1},{1,2},{2,3},{3,4},{4,5},{5,6},{6,7},{7,0},{8,9},{9,10},{10,1... | collective-permute-start | bytes 1572872 | tf_op jit(solution)/shard_map/ppermute | solution.py:41
  43.5 15.5 %collective-permute-start.1 = (bf16[256,256]{1,0:T(8,128)(2,1)S(1)}, bf16[256,256]{1,0:T(8,128)(2,1)S(1)}, u32[]{:S(2)}, u32[]{:S(2)}) collective-permute-start(bf16[256,256]{1,0:T(8,128)(2,1)S(1)} %get-tuple-element.17), channel_id=1, source_target_pairs={{0,6},{1,7},{2,0},{3,1},{4,2},{5,3},{6,4},{7,5},{8,14},{9,15},{10,... | collective-permute-start | bytes 393224 | tf_op jit(solution)/shard_map/ppermute | solution.py:41
  48.2 29.8 %collective-permute-start.4 = (bf16[256,256]{1,0:T(8,128)(2,1)S(1)}, bf16[256,256]{1,0:T(8,128)(2,1)S(1)}, u32[]{:S(2)}, u32[]{:S(2)}) collective-permute-start(bf16[256,256]{1,0:T(8,128)(2,1)S(1)} %get-tuple-element.16), channel_id=1, source_target_pairs={{0,2},{1,3},{2,4},{3,5},{4,6},{5,7},{6,0},{7,1},{8,10},{9,11},{10,... | collective-permute-start | bytes 393224 | tf_op jit(solution)/shard_map/ppermute | solution.py:41
  54.2 27.7 %all-to-all-start.1 = ((bf16[4,144,512]{2,1,0:T(8,128)(2,1)}), bf16[4,144,512]{2,1,0:T(8,128)(2,1)S(1)}, u32[]{:S(2)}, u32[]{:S(2)}) async-start(bf16[4,144,512]{2,1,0:T(8,128)(2,1)} %broadcast_in_dim.37), calls=%async_computation.2 | async-start | bytes 1179648 | tf_op jit(solution)/shard_map/all_to_all | solution.py:27
  59.0 21.9 %copy-start.6 = (s32[1152]{0:T(1024)S(1)}, s32[1152]{0:T(1024)}, u32[]{:S(2)}) copy-start(s32[1152]{0:T(1024)} %fusion.32) | copy-start | bytes 13828
  60.2 23.8 %collective-permute-start.6 = (bf16[512,256]{1,0:T(8,128)(2,1)S(1)}, bf16[512,256]{1,0:T(8,128)(2,1)S(1)}, u32[]{:S(2)}, u32[]{:S(2)}) collective-permute-start(bf16[512,256]{1,0:T(8,128)(2,1)S(1)} %add_convert_fusion.1), channel_id=1, source_target_pairs={{0,6},{1,7},{2,0},{3,1},{4,2},{5,3},{6,4},{7,5},{8,14},{9,15},{10,... | collective-permute-start | bytes 786440 | tf_op jit(solution)/shard_map/ppermute | solution.py:41
  79.0 2.8 %copy-start.4 = (f32[4096]{0:T(1024)S(1)}, f32[4096]{0:T(1024)}, u32[]{:S(2)}) copy-start(f32[4096]{0:T(1024)} %param.11) | copy-start | bytes 49156
  79.0 4.8 %copy-start.7 = (s32[8]{0:T(128)S(1)}, s32[8]{0:T(128)}, u32[]{:S(2)}) copy-start(s32[8]{0:T(128)} %param.8) | copy-start | bytes 100
  79.1 22.8 %collective-permute-start.5 = (bf16[512,256]{1,0:T(8,128)(2,1)S(1)}, bf16[512,256]{1,0:T(8,128)(2,1)S(1)}, u32[]{:S(2)}, u32[]{:S(2)}) collective-permute-start(bf16[512,256]{1,0:T(8,128)(2,1)S(1)} %add_convert_fusion.2), channel_id=1, source_target_pairs={{0,2},{1,3},{2,4},{3,5},{4,6},{5,7},{6,0},{7,1},{8,10},{9,11},{10,... | collective-permute-start | bytes 786440 | tf_op jit(solution)/shard_map/ppermute | solution.py:41
  82.0 21.6 %collective-permute-start = (bf16[576,512]{1,0:T(8,128)(2,1)S(1)}, bf16[576,512]{1,0:T(8,128)(2,1)S(1)}, u32[]{:S(2)}, u32[]{:S(2)}) collective-permute-start(bf16[576,512]{1,0:T(8,128)(2,1)S(1)} %bitcast.31), channel_id=1, source_target_pairs={{0,8},{8,0},{1,9},{9,1},{2,10},{10,2},{3,11},{11,3},{4,12},{12,4},... | collective-permute-start | bytes 1769480 | tf_op jit(solution)/shard_map/ppermute | solution.py:36
  104.6 12.4 %all-to-all-start.2 = ((f32[8,2,256]{2,1,0:T(2,128)}), f32[8,2,256]{2,1,0:T(2,128)S(1)}, u32[]{:S(2)}, u32[]{:S(2)}) async-start(f32[8,2,256]{2,1,0:T(2,128)} %broadcast_in_dim.38), calls=%async_computation.3 | async-start | bytes 32768 | tf_op jit(solution)/shard_map/all_to_all | solution.py:27
  117.5 3.9 %collective-permute-start.7 = (bf16[576,512]{1,0:T(8,128)(2,1)S(1)}, bf16[576,512]{1,0:T(8,128)(2,1)S(1)}, u32[]{:S(2)}, u32[]{:S(2)}) collective-permute-start(bf16[576,512]{1,0:T(8,128)(2,1)S(1)} %convolution_convert_fusion.3), channel_id=1, source_target_pairs={{0,8},{8,0},{1,9},{9,1},{2,10},{10,2},{3,11},{11,3},{4,12},{12,4},... | collective-permute-start | bytes 1769480 | tf_op jit(solution)/shard_map/ppermute | solution.py:36
  121.7 35.0 %copy-start.1 = (bf16[96,4096]{1,0:T(8,128)(2,1)S(1)}, bf16[96,4096]{1,0:T(8,128)(2,1)}, u32[]{:S(2)}) copy-start(bf16[96,4096]{1,0:T(8,128)(2,1)} %param.10) | copy-start | bytes 2359300
  156.7 1.7 %copy-start.2 = (bf16[96,4096]{1,0:T(8,128)(2,1)S(1)}, bf16[96,4096]{1,0:T(8,128)(2,1)}, u32[]{:S(2)}) copy-start(bf16[96,4096]{1,0:T(8,128)(2,1)} %reduce-scatter.2.cloned.1.call-done) | copy-start | bytes 2359300
Sparse Core Ops, SparseCore 0:
  18.6 115.3 reduce-scatter.1
